TPU v7x, 32 devices: a 4x4x1 block of a 4x4x8 slice. The times are simulated.
32 devices in a mesh: dp: 1 (over z), ep: 32 (over y, x, core).
Axes of the slice: x: 4, y: 4, z: 1, core: 2. Of those that a mesh axis runs over, the one named last changes fastest.
The devices are a block of a 4x4x8 slice.
Arguments:
- grad_y: bfloat16 [8192, 1024], P(('dp', 'ep'))
- gate_vals: float32 [8192, 8], P(('dp', 'ep'))
- topk_idx: int32 [8192, 8], P(('dp', 'ep'))
- slot_ids: int32 [8192, 8], P(('dp', 'ep'))
- pair_counts: int32 [32, 32], P(('dp', 'ep'))
- y_routed: bfloat16 [8192, 8, 1024], P(('dp', 'ep'))
- x_disp: bfloat16 [32, 4096, 1024], P(('dp', 'ep'))
- h_gate: bfloat16 [32, 4096, 512], P(('dp', 'ep'))
- h_up: bfloat16 [32, 4096, 512], P(('dp', 'ep'))
- w_gate: bfloat16 [32, 1024, 512], P('ep')
- w_up: bfloat16 [32, 1024, 512], P('ep')
- w_down: bfloat16 [32, 512, 1024], P('ep')
Outputs:
- output 1: bfloat16 [8192, 1024], P(('dp', 'ep'))
- output 2: float32 [8192, 8], P(('dp', 'ep'))
- output 3: float32 [32, 1024, 512], P(('dp', 'ep'))
- output 4: float32 [32, 1024, 512], P(('dp', 'ep'))
- output 5: float32 [32, 512, 1024], P(('dp', 'ep'))
All inputs are finite; a program needn't handle non-finite values.
Results may differ from a plain program's by a relative error of at most 0.0149524.
Values are sent between devices in bfloat16 or wider.
A program may use at most 768 MiB of HBM per device.

v0:
```python
import jax
import jax.numpy as jnp
from jax import lax
from jax.sharding import PartitionSpec as P


def build_send(grad_y, gate_vals, topk_idx, slot_ids, n_exp, cap_rows):
    tok_dev, top_k = topk_idx.shape
    dest_row = jnp.where(slot_ids >= 0, topk_idx * cap_rows + slot_ids, n_exp * cap_rows).reshape(-1)
    row_source = jnp.full((n_exp * cap_rows,), tok_dev * top_k, jnp.int32).at[dest_row].set(jnp.arange(tok_dev * top_k, dtype=jnp.int32), mode="drop")
    dy_rows = jnp.take(grad_y, row_source // top_k, axis=0, mode="fill", fill_value=0)
    gate_rows = jnp.take(gate_vals.reshape(-1), row_source, mode="fill", fill_value=0)
    return (gate_rows[:, None] * dy_rows).astype(jnp.bfloat16).reshape(n_exp, cap_rows, grad_y.shape[1])


def gather_back(ret_rows, topk_idx, slot_ids, cap_rows):
    tok_dev, top_k = topk_idx.shape
    src_row = jnp.where(slot_ids >= 0, topk_idx * cap_rows + slot_ids, ret_rows.shape[0]).reshape(-1)
    picked = jnp.take(ret_rows, src_row, axis=0, mode="fill", fill_value=0).reshape(tok_dev, top_k, ret_rows.shape[1])
    return jnp.sum(picked, axis=1, dtype=jnp.float32).astype(jnp.bfloat16)


def expert_grads(grad_rows, x_rows, hg_rows, hu_rows, w_gate, w_up, w_down):
    grad_hidden = jnp.einsum("erd,efd->erf", grad_rows, w_down, preferred_element_type=jnp.float32).astype(jnp.bfloat16)
    gate_f = hg_rows.astype(jnp.float32)
    up_f = hu_rows.astype(jnp.float32)
    gate_sig = jax.nn.sigmoid(gate_f)
    gate_act = gate_f * gate_sig
    hidden_act = (gate_act * up_f).astype(jnp.bfloat16)
    grad_h = grad_hidden.astype(jnp.float32)
    grad_hgate = (grad_h * up_f * gate_sig * (1.0 + gate_f * (1.0 - gate_sig))).astype(jnp.bfloat16)
    grad_hup = (grad_h * gate_act).astype(jnp.bfloat16)
    grad_wdown = jnp.einsum("erf,erd->efd", hidden_act, grad_rows, preferred_element_type=jnp.float32)
    grad_wgate = jnp.einsum("erd,erf->edf", x_rows, grad_hgate, preferred_element_type=jnp.float32)
    grad_wup = jnp.einsum("erd,erf->edf", x_rows, grad_hup, preferred_element_type=jnp.float32)
    grad_disp = (jnp.einsum("erf,edf->erd", grad_hgate, w_gate, preferred_element_type=jnp.float32) + jnp.einsum("erf,edf->erd", grad_hup, w_up, preferred_element_type=jnp.float32)).astype(jnp.bfloat16)
    return grad_disp, grad_wgate, grad_wup, grad_wdown


def solution(mesh):
    n_dev = mesh.shape["ep"]
    rows_spec = P(("dp", "ep"), None)
    cube_spec = P(("dp", "ep"), None, None)
    weight_spec = P("ep", None, None)

    def local_step(grad_y, gate_vals, topk_idx, slot_ids, pair_counts, y_routed, x_disp, h_gate, h_up, w_gate, w_up, w_down):
        n_loc = w_gate.shape[0]
        n_exp = n_loc * n_dev
        cap_rows = x_disp.shape[1] // n_dev
        model_dim = grad_y.shape[1]
        grad_gate = jnp.einsum("td,tkd->tk", grad_y, y_routed, preferred_element_type=jnp.float32)
        send_rows = build_send(grad_y, gate_vals, topk_idx, slot_ids, n_exp, cap_rows)
        recv_rows = lax.all_to_all(send_rows.reshape(n_dev, n_loc, cap_rows, model_dim), "ep", 0, 1)
        recv_counts = lax.all_to_all(pair_counts.reshape(n_dev, n_loc), "ep", 0, 1)
        keep_row = lax.broadcasted_iota(jnp.int32, (n_loc, n_dev, cap_rows), 2) < recv_counts[:, :, None]
        grad_rows = jnp.where(keep_row[..., None], recv_rows, jnp.zeros((), jnp.bfloat16)).reshape(n_loc, n_dev * cap_rows, model_dim)
        grad_disp, grad_wgate, grad_wup, grad_wdown = expert_grads(grad_rows, x_disp, h_gate, h_up, w_gate, w_up, w_down)
        ret_rows = lax.all_to_all(grad_disp.reshape(n_loc, n_dev, cap_rows, model_dim), "ep", 1, 0)
        grad_x = gather_back(ret_rows.reshape(n_exp * cap_rows, model_dim), topk_idx, slot_ids, cap_rows)
        return grad_x, grad_gate, grad_wgate, grad_wup, grad_wdown

    return jax.shard_map(local_step, mesh=mesh, in_specs=(rows_spec, rows_spec, rows_spec, rows_spec, rows_spec, cube_spec, cube_spec, cube_spec, cube_spec, weight_spec, weight_spec, weight_spec), out_specs=(rows_spec, rows_spec, cube_spec, cube_spec, cube_spec), check_vma=False)
```

profile of v0, /device:TPU:103, one launch (start us, length us, event | category | flops | bytes accessed | tf_op | source)
XLA Modules:
  0.0 363.4 jit_solution(7078524115895638918)
XLA Ops:
  0.6 0.0 copy-start
  0.6 1.4 copy.34
  2.1 8.0 %all-to-all-start = ((s32[32,1,1]{2,1,0:T(1,128)}), s32[32,1,1]{2,1,0:T(1,128)S(1)}, u32[]{:S(2)}, u32[]{:S(2)}) async-start(s32[32,1,1]{2,1,0:T(1,128)} %copy.34), calls=%async_computation | async-start | bytes 32768 | tf_op jit(solution)/shard_map/all_to_all | solution.py:54
  10.1 0.7 compare_and_fusion
  10.8 0.1 copy.35
  10.9 0.1 reshape.221
  11.1 8.1 %scatter_custom_fusion = s32[4096]{0:T(1024)S(1)} fusion(s32[2048]{0:T(1024)S(1)} %bitcast.78, s32[2048]{0:T(1024)S(1)} %iota.11, s32[]{:T(128)} %constant.61.clone.1), kind=kCustom, calls=%fused_computation.60 | custom fusion | bytes 16388 | tf_op jit(solution)/shard_map/scatter | solution.py:10
  19.2 0.8 copy.36
  20.0 0.1 reshape.222
  20.2 0.0 copy-start.2
  20.2 23.0 %gather_fusion = f32[4096]{0:T(1024)S(1)} fusion(f32[2048]{0:T(1024)S(1)} %reshape.222, s32[4096]{0:T(1024)S(1)} %get-tuple-element.27), kind=kCustom, calls=%fused_computation | custom fusion | bytes 49152 | tf_op jit(solution)/shard_map/jit(_take)/gather | solution.py:12
  43.2 0.0 copy-done.2
  43.2 18.2 %gather_fusion.1 = bf16[4096,1024]{1,0:T(8,128)(2,1)} fusion(bf16[256,1024]{1,0:T(8,128)(2,1)S(1)} %copy-done.2, s32[4096]{0:T(1024)S(1)} %get-tuple-element.28), kind=kCustom, calls=%fused_computation.1 | custom fusion | bytes 16793600 | tf_op jit(solution)/shard_map/jit(_take)/gather | solution.py:11
  61.5 7.8 %multiply_convert_fusion = bf16[32,1,1,128,1024]{4,3,2,1,0:T(8,128)(2,1)} fusion(bf16[32,1,1,128,1024]{4,3,2,1,0:T(8,128)(2,1)} %bitcast.74, f32[32,128]{1,0:T(8,128)S(1)} %select_bitcast_fusion, pred[32,128]{1,0:T(8,128)(4,1)S(1)} %and_bitcast_fusion), kind=kLoop, calls=%fused_computation.5 | loop fusion | flops 16777216 | bytes 16797696 | tf_op jit(solution)/shard_map/convert_element_type | solution.py:13
  69.3 0.0 all-to-all-done
  69.3 6.3 %all-to-all-start.1 = ((bf16[32,1,1,128,1024]{4,3,2,1,0:T(8,128)(2,1)}), bf16[32,1,1,128,1024]{4,3,2,1,0:T(8,128)(2,1)}, u32[]{:S(2)}, u32[]{:S(2)}) async-start(bf16[32,1,1,128,1024]{4,3,2,1,0:T(8,128)(2,1)} %multiply_convert_fusion), calls=%async_computation.1 | async-start | bytes 16777216 | tf_op jit(solution)/shard_map/all_to_all | solution.py:53
  75.7 0.7 reduce.1
  76.3 0.1 iota_compare_fusion
  76.4 112.4 %all-to-all-done.1 = bf16[32,1,1,128,1024]{4,3,2,1,0:T(8,128)(2,1)} async-done(((bf16[32,1,1,128,1024]{4,3,2,1,0:T(8,128)(2,1)}), bf16[32,1,1,128,1024]{4,3,2,1,0:T(8,128)(2,1)}, u32[]{:S(2)}, u32[]{:S(2)}) %all-to-all-start.1) | async-done | bytes 8388640 | tf_op jit(solution)/shard_map/all_to_all | solution.py:53
  188.8 0.0 copy-start.4
  188.8 0.0 copy-start.5
  188.8 5.8 %broadcast_select_fusion = bf16[32,1,1,128,1024]{4,3,2,1,0:T(8,128)(2,1)S(1)} fusion(bf16[32,1,1,128,1024]{4,3,2,1,0:T(8,128)(2,1)} %all-to-all-done.1, pred[32,128]{1,0:T(8,128)(4,1)S(1)} %iota_compare_fusion), kind=kLoop, calls=%fused_computation.25 | loop fusion | flops 4194304 | bytes 16781312 | tf_op jit(solution)/shard_map/jit(_where)/select_n | solution.py:56
  194.6 0.0 copy-start.3
  194.6 0.0 copy-done
  194.6 0.0 copy-done.4
  194.6 0.1 copy-done.5
  194.8 0.0 copy-start.6
  194.8 9.5 %fusion.3 = (bf16[1,4096,512]{2,1,0:T(8,128)(2,1)}, bf16[1,4096,512]{2,1,0:T(8,128)(2,1)}) fusion(bf16[1,4096,512]{2,1,0:T(8,128)(2,1)S(1)} %copy-done.4, bf16[1,4096,512]{2,1,0:T(8,128)(2,1)S(1)} %copy-done.5, bf16[4096,1024]{1,0:T(8,128)(2,1)S(1)} %bitcast.75, bf16[1,512,1024]{2,1,0:T(8,128)(2,1)S(1)} %copy-done), kind=kOutput, calls=%fused_computation.15 | convolution fusion | flops 4324327424 | bytes 26214400 | tf_op jit(solution)/shard_map/erd,efd->erf/dot_general | solution.py:24
  204.2 0.0 copy-done.3
  204.2 0.0 copy-done.6
  204.2 0.0 copy-start.7
  204.2 10.5 %fusion.20 = f32[4096,1024]{1,0:T(8,128)} fusion(bf16[1,4096,512]{2,1,0:T(8,128)(2,1)} %get-tuple-element.29, bf16[1,1024,512]{2,1,0:T(8,128)(2,1)S(1)} %copy-done.6), kind=kOutput, calls=%fused_computation.34 | convolution fusion | flops 4294967296 | bytes 22020096 | tf_op jit(solution)/shard_map/erf,edf->erd/dot_general | solution.py:36
  214.7 0.0 copy-done.7
  214.7 11.8 %add_convert_fusion = bf16[4096,1024]{1,0:T(8,128)(2,1)} fusion(f32[4096,1024]{1,0:T(8,128)} %fusion.20, bf16[1,1024,512]{2,1,0:T(8,128)(2,1)S(1)} %copy-done.7, bf16[1,4096,512]{2,1,0:T(8,128)(2,1)} %get-tuple-element.30, bf16[1,4096,512]{2,1,0:T(8,128)(2,1)S(1)} %copy-done.5), kind=kOutput, calls=%fused_computation.4 | convolution fusion | flops 4320133120 | bytes 34603008 | tf_op jit(solution)/shard_map/erf,edf->erd/dot_general | solution.py:36
  226.5 4.1 %all-to-all-start.2 = ((bf16[1,1,32,128,1024]{4,3,1,0,2:T(8,128)(2,1)}), bf16[1,1,32,128,1024]{4,3,1,0,2:T(8,128)(2,1)}, u32[]{:S(2)}, u32[]{:S(2)}) async-start(bf16[1,1,32,128,1024]{4,3,1,0,2:T(8,128)(2,1)} %bitcast.77), calls=%async_computation.2 | async-start | bytes 16777216 | tf_op jit(solution)/shard_map/all_to_all | solution.py:58
  230.6 0.2 copy.33
  230.8 4.8 %fusion.36 = f32[256,1,8]{2,1,0:T(1,128)S(1)} fusion(bf16[256,8,1024]{2,1,0:T(8,128)(2,1)} %param.17, bf16[256,1024,1]{1,0,2:T(8,128)(2,1)S(1)} %bitcast.73), kind=kOutput, calls=%fused_computation.42 | convolution fusion | flops 4194304 | bytes 4726784 | tf_op jit(solution)/shard_map/td,tkd->tk/dot_general | solution.py:51
  235.6 0.7 copy.42
  236.3 8.2 %fusion.25 = f32[1,1024,512]{1,2,0:T(8,128)S(1)} fusion(bf16[1,4096,1024]{2,1,0:T(8,128)(2,1)} %param.18, bf16[1,4096,512]{2,1,0:T(8,128)(2,1)} %get-tuple-element.29), kind=kOutput, calls=%fused_computation.37 | convolution fusion | flops 4294967296 | bytes 14680064 | tf_op jit(solution)/shard_map/erd,erf->edf/dot_general | solution.py:34
  244.5 1.8 copy.39
  246.3 9.8 %fusion.30 = f32[1,1024,512]{1,2,0:T(8,128)S(1)} fusion(bf16[1,4096,1024]{2,1,0:T(8,128)(2,1)} %param.18, bf16[1,4096,512]{2,1,0:T(8,128)(2,1)} %get-tuple-element.30, bf16[1,4096,512]{2,1,0:T(8,128)(2,1)} %param.19), kind=kOutput, calls=%fused_computation.38 | convolution fusion | flops 4311744512 | bytes 18874368 | tf_op jit(solution)/shard_map/erd,erf->edf/dot_general | solution.py:35
  256.2 1.8 copy.40
  258.0 11.9 %fusion.22 = f32[1,512,1024]{2,1,0:T(8,128)} fusion(bf16[4096,1024]{1,0:T(8,128)(2,1)} %bitcast.76, bf16[1,4096,512]{2,1,0:T(8,128)(2,1)} %param.20, bf16[1,4096,512]{2,1,0:T(8,128)(2,1)} %param.19), kind=kOutput, calls=%fused_computation.36 | convolution fusion | flops 4311744512 | bytes 18874368 | tf_op jit(solution)/shard_map/erf,erd->efd/dot_general | solution.py:33
  269.9 73.1 %all-to-all-done.2 = bf16[1,1,32,128,1024]{4,3,1,0,2:T(8,128)(2,1)} async-done(((bf16[1,1,32,128,1024]{4,3,1,0,2:T(8,128)(2,1)}), bf16[1,1,32,128,1024]{4,3,1,0,2:T(8,128)(2,1)}, u32[]{:S(2)}, u32[]{:S(2)}) %all-to-all-start.2) | async-done | bytes 8388640 | tf_op jit(solution)/shard_map/all_to_all | solution.py:58
  343.0 0.0 copy-start.1
  343.0 15.5 %gather_fusion.2 = bf16[2048,1024]{1,0:T(8,128)(2,1)} fusion(bf16[4096,1024]{1,0:T(8,128)(2,1)} %bitcast.16, s32[2048]{0:T(1024)S(1)} %broadcast_clamp_fusion.1), kind=kCustom, calls=%fused_computation.2 | custom fusion | bytes 8396800 | tf_op jit(solution)/shard_map/jit(_take)/gather | solution.py:19
  358.5 4.9 %fusion.18 = bf16[256,1024]{1,0:T(8,128)(2,1)} fusion(bf16[2048,1024]{1,0:T(8,128)(2,1)} %gather_fusion.2, pred[256,8]{1,0:T(8,128)(4,1)S(1)} %copy.33), kind=kLoop, calls=%fused_computation.32 | loop fusion | flops 3932160 | bytes 4720640 | tf_op jit(solution)/shard_map/reduce_sum | solution.py:20
  363.4 0.0 copy-done.1
  (6 shorter events, 0.1 us)
Async XLA Ops:
  0.6 194.0 %copy-start = (bf16[1,512,1024]{2,1,0:T(8,128)(2,1)S(1)}, bf16[1,512,1024]{2,1,0:T(8,128)(2,1)}, u32[]{:S(2)}) copy-start(bf16[1,512,1024]{2,1,0:T(8,128)(2,1)} %param.23) | copy-start | bytes 3145732
  2.1 67.2 %all-to-all-start = ((s32[32,1,1]{2,1,0:T(1,128)}), s32[32,1,1]{2,1,0:T(1,128)S(1)}, u32[]{:S(2)}, u32[]{:S(2)}) async-start(s32[32,1,1]{2,1,0:T(1,128)} %copy.34), calls=%async_computation | async-start | bytes 32768 | tf_op jit(solution)/shard_map/all_to_all | solution.py:54
  20.2 23.1 %copy-start.2 = (bf16[256,1024]{1,0:T(8,128)(2,1)S(1)}, bf16[256,1024]{1,0:T(8,128)(2,1)}, u32[]{:S(2)}) copy-start(bf16[256,1024]{1,0:T(8,128)(2,1)} %param.12) | copy-start | bytes 1572868
  69.3 119.5 %all-to-all-start.1 = ((bf16[32,1,1,128,1024]{4,3,2,1,0:T(8,128)(2,1)}), bf16[32,1,1,128,1024]{4,3,2,1,0:T(8,128)(2,1)}, u32[]{:S(2)}, u32[]{:S(2)}) async-start(bf16[32,1,1,128,1024]{4,3,2,1,0:T(8,128)(2,1)} %multiply_convert_fusion), calls=%async_computation.1 | async-start | bytes 16777216 | tf_op jit(solution)/shard_map/all_to_all | solution.py:53
  188.8 5.8 %copy-start.4 = (bf16[1,4096,512]{2,1,0:T(8,128)(2,1)S(1)}, bf16[1,4096,512]{2,1,0:T(8,128)(2,1)}, u32[]{:S(2)}) copy-start(bf16[1,4096,512]{2,1,0:T(8,128)(2,1)} %param.20) | copy-start | bytes 12582916
  188.8 6.0 %copy-start.5 = (bf16[1,4096,512]{2,1,0:T(8,128)(2,1)S(1)}, bf16[1,4096,512]{2,1,0:T(8,128)(2,1)}, u32[]{:S(2)}) copy-start(bf16[1,4096,512]{2,1,0:T(8,128)(2,1)} %param.19) | copy-start | bytes 12582916
  194.6 9.6 %copy-start.3 = (bf16[32,1,1,128,1024]{4,3,2,1,0:T(8,128)(2,1)}, bf16[32,1,1,128,1024]{4,3,2,1,0:T(8,128)(2,1)S(1)}, u32[]{:S(2)}) copy-start(bf16[32,1,1,128,1024]{4,3,2,1,0:T(8,128)(2,1)S(1)} %broadcast_select_fusion) | copy-start | bytes 25165828
  194.8 9.5 %copy-start.6 = (bf16[1,1024,512]{2,1,0:T(8,128)(2,1)S(1)}, bf16[1,1024,512]{2,1,0:T(8,128)(2,1)}, u32[]{:S(2)}) copy-start(bf16[1,1024,512]{2,1,0:T(8,128)(2,1)} %param.21) | copy-start | bytes 3145732
  204.2 10.5 %copy-start.7 = (bf16[1,1024,512]{2,1,0:T(8,128)(2,1)S(1)}, bf16[1,1024,512]{2,1,0:T(8,128)(2,1)}, u32[]{:S(2)}) copy-start(bf16[1,1024,512]{2,1,0:T(8,128)(2,1)} %param.22) | copy-start | bytes 3145732
  226.5 116.4 %all-to-all-start.2 = ((bf16[1,1,32,128,1024]{4,3,1,0,2:T(8,128)(2,1)}), bf16[1,1,32,128,1024]{4,3,1,0,2:T(8,128)(2,1)}, u32[]{:S(2)}, u32[]{:S(2)}) async-start(bf16[1,1,32,128,1024]{4,3,1,0,2:T(8,128)(2,1)} %bitcast.77), calls=%async_computation.2 | async-start | bytes 16777216 | tf_op jit(solution)/shard_map/all_to_all | solution.py:58
  343.0 20.5 %copy-start.1 = (bf16[1,512,1024]{2,1,0:T(8,128)(2,1)S(1)}, bf16[1,512,1024]{2,1,0:T(8,128)(2,1)}, u32[]{:S(2)}) copy-start(bf16[1,512,1024]{2,1,0:T(8,128)(2,1)} %param.23) | copy-start | bytes 3145732
where the time goes:
time: 364 us; the launch traced here: 363 us
  waiting for transfers between devices  185 us (51%)
  local copies, waits for them, and re-layouts  72.1 us (20%)
  matrix products  66.5 us (18%)
  other arithmetic  20.1 us (6%)
  starting transfers between devices  18.4 us (5%)
    all_to_all x1, waiting for transfers between devices, local_step(): lax.all_to_all(send_rows.reshape(n_dev, n_loc, cap_rows, model_dim), 'ep'...  112 us
    all_to_all x1, waiting for transfers between devices, local_step(): lax.all_to_all(grad_disp.reshape(n_loc, n_dev, cap_rows, model_dim), 'ep'...  73.1 us
    gather x1, local copies, waits for them, and re-layouts, build_send(): jnp.take(gate_vals.reshape(-1), row_source, mode='fill', fill_value=0)  23 us
    gather x1, local copies, waits for them, and re-layouts, build_send(): jnp.take(grad_y, row_source // top_k, axis=0, mode='fill', fill_value=0)  18.2 us
    gather x1, local copies, waits for them, and re-layouts, gather_back(): jnp.take(ret_rows, src_row, axis=0, mode='fill', fill_value=0)  15.5 us
    dot_general x1, matrix products, expert_grads(): jnp.einsum('erf,erd->efd', hidden_act, grad_rows, preferred_element_type=...  11.9 us
    dot_general x1, matrix products, expert_grads(): jnp.einsum('erf,edf->erd', grad_hup, w_up, preferred_element_type=jnp.flo...  11.8 us
    dot_general x1, matrix products, expert_grads(): jnp.einsum('erf,edf->erd', grad_hgate, w_gate, preferred_element_type=jnp...  10.5 us
  transfers between devices with their start and end apart: 3, of which 2 were waited for; matrix products, arithmetic and copies ran while one was open for 27% of the time, Pallas kernels for 0%

commit v1 on v0

v1 whole, which is shorter than its diff:
```python
import functools
import math

import jax
import jax.numpy as jnp
from jax import lax
from jax.experimental import pallas as pl
from jax.experimental.pallas import tpu as pltpu
from jax.sharding import PartitionSpec as P

MESH = pl.DeviceIdType.MESH
CORES = 2
BF16, F32 = jnp.bfloat16, jnp.float32

ORDER = ((0, 0), (-1, 0), (1, 0), (0, -1), (0, 1), (2, 0), (0, 2), (-1, -1), (1, 1), (-1, 1), (1, -1), (2, -1), (-1, 2), (2, 1), (1, 2), (2, 2))

NN = (((1,), (0,)), ((), ()))
NT = (((1,), (1,)), ((), ()))
TN = (((0,), (0,)), ((), ()))


def dot(a, b, dims):
    return lax.dot_general(a, b, dims, preferred_element_type=F32)


def lut(k, vals):
    out = vals[0]
    for i, v in enumerate(vals):
        if i:
            out = jnp.where(k == i, v, out)
    return out


def kernel(n_dev, side, gy_ref, tab_ref, own_ref, x_ref, hg_ref, hu_ref, wg_ref, wu_ref, wd_ref,
           gx_ref, gwg_ref, gwu_ref, gwd_ref,
           tokens, tabs, rbuf, ret, wgu, wd, xb, hgb, hub, gacc,
           tok_sem, tab_sem, ret_sem, ag_send, pair_send, tab_send, ret_send, load_sem, w_sem, loc_sem):
    me = lax.axis_index("ep")
    core = me % CORES
    mx = (me // CORES) % side
    my = me // (CORES * side)
    tok_dev, model_dim = gy_ref.shape
    ffn = wg_ref.shape[1]
    cap = rbuf.shape[1]
    half = tok_dev // 2
    n_chip = side * side
    crow = CORES * cap

    def plane(a, b):
        x = (mx + (1 - core) * a + core * b + 2 * side) % side
        y = (my + core * a + (1 - core) * b + 2 * side) % side
        return (y * side + x) * CORES + core

    partner = me + 1 - 2 * core

    barrier = pltpu.get_barrier_semaphore()

    def signal_one(i, carry):
        pl.semaphore_signal(barrier, inc=1, device_id={"ep": (me + 1 + i) % n_dev}, device_id_type=MESH)
        return carry

    lax.fori_loop(0, n_dev - 1, signal_one, 0)

    wcopies = [
        pltpu.make_async_copy(wd_ref, wd, w_sem.at[0]),
        pltpu.make_async_copy(wg_ref, wgu.at[:, pl.ds(0, ffn)], w_sem.at[1]),
        pltpu.make_async_copy(wu_ref, wgu.at[:, pl.ds(ffn, ffn)], w_sem.at[2]),
    ]
    for c in wcopies:
        c.start()
    own_copy = pltpu.make_async_copy(gy_ref, tokens.at[me], tok_sem.at[me, 0])
    own_copy.start()
    tab_copy = pltpu.make_async_copy(tab_ref.at[me], tabs.at[me], tab_sem.at[me])
    tab_copy.start()

    def chip_at(k, sign):
        dx = lut(k, [o[0] for o in ORDER])
        dy = lut(k, [o[1] for o in ORDER])
        x = (mx + sign * dx + 2 * side) % side
        y = (my + sign * dy + 2 * side) % side
        return y * side + x

    def loads(k):
        q = chip_at(k, 1)
        slot = k % 2
        rows = pl.ds(pl.multiple_of(q * crow, crow), crow)
        return [
            pltpu.make_async_copy(x_ref.at[rows], xb.at[slot], load_sem.at[0, slot]),
            pltpu.make_async_copy(hg_ref.at[rows], hgb.at[slot], load_sem.at[1, slot]),
            pltpu.make_async_copy(hu_ref.at[rows], hub.at[slot], load_sem.at[2, slot]),
        ]

    for c in loads(0):
        c.start()
    gwg_ref[...] = jnp.zeros_like(gwg_ref)
    gwu_ref[...] = jnp.zeros_like(gwu_ref)
    gwd_ref[...] = jnp.zeros_like(gwd_ref)
    gacc[...] = jnp.zeros_like(gacc)
    pl.semaphore_wait(barrier, n_dev - 1)

    def tab_msg(i):
        to = (me + 1 + i) % n_dev
        return pltpu.make_async_remote_copy(src_ref=tab_ref.at[to], dst_ref=tabs.at[me], send_sem=tab_send.at[i], recv_sem=tab_sem.at[me], device_id={"ep": to}, device_id_type=MESH)

    def tab_start(i, carry):
        tab_msg(i).start()
        return carry

    lax.fori_loop(0, n_dev - 1, tab_start, 0)

    sends, pairs = [], []

    def block(src, part):
        if part == "full":
            return tokens.at[src]
        return tokens.at[src, pl.ds(part * half, half)]

    def forward_msg(n, i, j, part, a, b):
        src = plane(i, j)
        ref = gy_ref if i == 0 and j == 0 else block(src, part)
        return pltpu.make_async_remote_copy(src_ref=ref, dst_ref=block(src, part), send_sem=ag_send.at[n], recv_sem=tok_sem.at[src, 1 if part == 1 else 0], device_id={"ep": plane(a, b)}, device_id_type=MESH)

    def forward(*what):
        what = (len(sends), *what)
        sends.append(what)
        forward_msg(*what).start()

    def pair_msg(n, i, j):
        src = plane(i, j)
        ref = gy_ref if i == 0 and j == 0 else tokens.at[src]
        return pltpu.make_async_remote_copy(src_ref=ref, dst_ref=tokens.at[src], send_sem=pair_send.at[n], recv_sem=tok_sem.at[src, 0], device_id={"ep": partner}, device_id_type=MESH)

    def to_partner(i, j):
        what = (len(pairs), i, j)
        pairs.append(what)
        pair_msg(*what).start()

    def arrived(src, part):
        ref = block(src, part)
        pltpu.make_async_copy(ref, ref, tok_sem.at[src, 1 if part == 1 else 0]).wait()

    to_partner(0, 0)
    for a, b in ((1, 0), (-1, 0), (0, 1), (0, -1)):
        forward(0, 0, "full", a, b)
    own_copy.wait()

    def event(i, j):
        src = plane(i, j)
        if i == 2 and j == 0 or j == 2:
            arrived(src, 0)
            arrived(src, 1)
        else:
            arrived(src, "full")
        if j == 0:
            if i == -1:
                forward(i, j, 0, 1, 0)
            if i == 1:
                forward(i, j, 1, -1, 0)
            forward(i, j, "full", 0, 1)
            forward(i, j, "full", 0, -1)
        elif j == -1:
            forward(i, j, 0, 0, 1)
        elif j == 1:
            forward(i, j, 1, 0, -1)
        to_partner(i, j)

    events = {
        1: ((-1, 0), (1, 0), (0, -1), (0, 1)),
        3: ((2, 0), (0, 2)),
        5: ((-1, -1), (-1, 1), (1, -1), (1, 1)),
        7: ((2, -1), (2, 1)),
        9: ((-1, 2), (1, 2)),
        10: ((2, 2),),
    }

    def ret_msg(k, cc):
        q = chip_at(k, 1)
        to = q * CORES + cc
        return pltpu.make_async_remote_copy(src_ref=rbuf.at[to], dst_ref=ret.at[me], send_sem=ret_send.at[to], recv_sem=ret_sem.at[me], device_id={"ep": to}, device_id_type=MESH)

    def local_ret():
        return pltpu.make_async_copy(rbuf.at[me], ret.at[me], ret_sem.at[me])

    def send_chunk(k):
        @pl.when(k == 0)
        def _():
            local_ret().start()
            to = partner
            pltpu.make_async_remote_copy(src_ref=rbuf.at[to], dst_ref=ret.at[me], send_sem=ret_send.at[to], recv_sem=ret_sem.at[me], device_id={"ep": to}, device_id_type=MESH).start()

        @pl.when(k > 0)
        def _():
            for cc in range(CORES):
                ret_msg(k, cc).start()

    slot_iota = lax.broadcasted_iota(jnp.int32, (cap, tok_dev), 0).astype(F32)
    for c in wcopies:
        c.wait()

    def chunk(k, carry):
        for at, evs in events.items():
            @pl.when(k == at)
            def _(evs=evs):
                for i, j in evs:
                    event(i, j)

        @pl.when(k > 0)
        def _():
            send_chunk(k - 1)

        slot = k % 2
        for c in loads(k):
            c.wait()

        @pl.when(k + 1 < n_chip)
        def _():
            for c in loads(k + 1):
                c.start()

        q = chip_at(k, 1)
        @pl.when(k > 0)
        def _():
            src = q * CORES + 1 - core
            arrived(src, "full")

        @pl.when(k == 0)
        def _():
            arrived(partner, "full")

        d_parts = []
        for cc in range(CORES):
            home = q * CORES + cc
            pltpu.make_async_copy(tabs.at[home], tabs.at[home], tab_sem.at[home]).wait()
            tab = tabs[home]
            pick = tab[0:1, :] == slot_iota
            gate = jnp.sum(jnp.where(pick, tab[1:2, :], 0.0), axis=1, keepdims=True)
            rows = dot(pick.astype(F32).astype(BF16), tokens[home], NN)
            d_parts.append((gate * rows).astype(BF16))
        d = jnp.concatenate(d_parts, axis=0)
        da = dot(d, wd[...], NT).astype(BF16).astype(F32)
        h1 = hgb[slot].astype(F32)
        h3 = hub[slot].astype(F32)
        g = jax.nn.sigmoid(h1)
        s = h1 * g
        act = (s * h3).astype(BF16)
        dh1 = (da * h3 * g * (1.0 + h1 * (1.0 - g))).astype(BF16)
        dh3 = (da * s).astype(BF16)
        dh = jnp.concatenate([dh1, dh3], axis=1)
        r = dot(dh, wgu[...], NT).astype(BF16)
        for cc in range(CORES):
            rbuf[q * CORES + cc] = r[cc * cap:(cc + 1) * cap]
        x = xb[slot]
        gwg_ref[...] += dot(x, dh1, TN)
        gwu_ref[...] += dot(x, dh3, TN)
        gwd_ref[...] += dot(act, d, TN)
        return carry

    lax.fori_loop(0, n_chip, chunk, 0)
    send_chunk(jnp.int32(n_chip - 1))

    def combine(k, carry):
        q = chip_at(k, -1)
        picks = []
        for cc in range(CORES):
            e = q * CORES + cc
            pltpu.make_async_copy(ret.at[e], ret.at[e], ret_sem.at[e]).wait()
            picks.append((own_ref[e] == slot_iota).astype(F32).astype(BF16))
        pick = jnp.concatenate(picks, axis=0)
        rows = jnp.concatenate([ret[q * CORES + cc] for cc in range(CORES)], axis=0)
        gacc[...] += dot(pick, rows, TN)
        return carry

    lax.fori_loop(0, n_chip, combine, 0)
    gx_ref[...] = gacc[...].astype(gx_ref.dtype)

    for what in sends:
        forward_msg(*what).wait_send()
    for what in pairs:
        pair_msg(*what).wait_send()

    def tab_done(i, carry):
        tab_msg(i).wait_send()
        return carry

    lax.fori_loop(0, n_dev - 1, tab_done, 0)

    def ret_done(i, carry):
        to = (me + 1 + i) % n_dev
        pltpu.make_async_remote_copy(src_ref=rbuf.at[to], dst_ref=ret.at[me], send_sem=ret_send.at[to], recv_sem=ret_sem.at[me], device_id={"ep": to}, device_id_type=MESH).wait_send()
        return carry

    lax.fori_loop(0, n_dev - 1, ret_done, 0)


def routing_tables(gate_vals, topk_idx, slot_ids, pair_counts, n_exp):
    ids = topk_idx.T
    slots = slot_ids.T
    gates = gate_vals.T
    expert = lax.broadcasted_iota(jnp.int32, (n_exp, ids.shape[1]), 0)
    slot_of = jnp.full((n_exp, ids.shape[1]), -1, jnp.int32)
    gate_of = jnp.zeros((n_exp, ids.shape[1]), F32)
    for j in range(ids.shape[0]):
        hit = ids[j][None, :] == expert
        slot_of = jnp.where(hit, slots[j][None, :], slot_of)
        gate_of = jnp.where(hit, gates[j][None, :], gate_of)
    real = slot_of < pair_counts.reshape(n_exp, 1)
    slot_d = jnp.where(real, slot_of, -1)
    return jnp.stack([slot_d.astype(F32), gate_of], axis=1), slot_of.astype(F32)[:, None, :]


def solution(mesh):
    n_dev = mesh.shape["ep"]
    side = math.isqrt(n_dev // CORES)
    rows_spec = P(("dp", "ep"), None)
    cube_spec = P(("dp", "ep"), None, None)
    weight_spec = P("ep", None, None)

    def local_step(grad_y, gate_vals, topk_idx, slot_ids, pair_counts, y_routed, x_disp, h_gate, h_up, w_gate, w_up, w_down):
        assert w_gate.shape[0] == 1
        assert side * side * CORES == n_dev and len(ORDER) == side * side
        cap = x_disp.shape[1] // n_dev
        tok_dev, model_dim = grad_y.shape
        ffn = w_gate.shape[2]
        crow = CORES * cap
        n_chip = side * side
        grad_gate = jnp.einsum("td,tkd->tk", grad_y, y_routed, preferred_element_type=F32)
        tab, own = routing_tables(gate_vals, topk_idx, slot_ids, pair_counts, n_dev)
        vmem = pl.BlockSpec(memory_space=pltpu.VMEM)
        anym = pl.BlockSpec(memory_space=pl.ANY)
        dma = pltpu.SemaphoreType.DMA
        gx, gwg, gwu, gwd = pl.pallas_call(
            functools.partial(kernel, n_dev, side),
            out_shape=(
                jax.ShapeDtypeStruct((tok_dev, model_dim), BF16),
                jax.ShapeDtypeStruct((model_dim, ffn), F32),
                jax.ShapeDtypeStruct((model_dim, ffn), F32),
                jax.ShapeDtypeStruct((ffn, model_dim), F32),
            ),
            in_specs=[vmem, vmem, vmem, anym, anym, anym, anym, anym, anym],
            out_specs=(vmem, vmem, vmem, vmem),
            scratch_shapes=[
                pltpu.VMEM((n_dev, tok_dev, model_dim), BF16),
                pltpu.VMEM((n_dev, 2, tok_dev), F32),
                pltpu.VMEM((n_dev, cap, model_dim), BF16),
                pltpu.VMEM((n_dev, cap, model_dim), BF16),
                pltpu.VMEM((model_dim, 2 * ffn), BF16),
                pltpu.VMEM((ffn, model_dim), BF16),
                pltpu.VMEM((2, crow, model_dim), BF16),
                pltpu.VMEM((2, crow, ffn), BF16),
                pltpu.VMEM((2, crow, ffn), BF16),
                pltpu.VMEM((tok_dev, model_dim), F32),
                dma((n_dev, 2)),
                dma((n_dev,)),
                dma((n_dev,)),
                dma((32,)),
                dma((n_chip,)),
                dma((n_dev,)),
                dma((n_dev,)),
                dma((3, 2)),
                dma((3,)),
                dma((1,)),
            ],
            compiler_params=pltpu.CompilerParams(collective_id=0, has_side_effects=True, vmem_limit_bytes=67043328),
            name="moe_bwd",
        )(grad_y, tab, own, x_disp[0], h_gate[0], h_up[0], w_gate[0], w_up[0], w_down[0])
        return gx, grad_gate, gwg[None], gwu[None], gwd[None]

    return jax.shard_map(local_step, mesh=mesh, in_specs=(rows_spec, rows_spec, rows_spec, rows_spec, rows_spec, cube_spec, cube_spec, cube_spec, cube_spec, weight_spec, weight_spec, weight_spec), out_specs=(rows_spec, rows_spec, cube_spec, cube_spec, cube_spec), check_vma=False)
```

time: 364 us -> 193 us (0.53)
  the two profiles are of different devices: /device:TPU:103 before, /device:TPU:97 now
where the time goes in v1:
time: 193 us
  Pallas kernels  175 us (91%)
  local copies, waits for them, and re-layouts  10.3 us (5%)
  matrix products  5.06 us (3%)
  other arithmetic  2.36 us (1%)
    pallas_call x1, Pallas kernels, local_step(): pl.pallas_call(functools.partial(kernel, n_dev, side), out_shape=(jax.Sha...  175 us
    unnamed x10, local copies, waits for them, and re-layouts  6.67 us
    dot_general x1, matrix products, local_step(): jnp.einsum('td,tkd->tk', grad_y, y_routed, preferred_element_type=F32)  5.06 us

profile of v1, /device:TPU:97, one launch (start us, length us, event | category | flops | bytes accessed | tf_op | source)
XLA Modules:
  0.0 193.0 jit_solution(7923942885767483434)
XLA Ops:
  0.6 1.0 fusion.5
  1.6 1.0 fusion.4
  2.6 0.8 fusion.3
  3.4 0.8 fusion.2
  4.2 1.0 fusion.6
  5.2 0.1 compare_select_fusion.15
  5.3 0.7 pad_maximum_fusion.tab_ref
  6.0 174.5 %moe_bwd.1 = (bf16[256,1024]{1,0:T(8,128)(2,1)}, f32[1024,512]{1,0:T(8,128)}, f32[1024,512]{1,0:T(8,128)}, f32[512,1024]{1,0:T(8,128)}) custom-call(bf16[256,1024]{1,0:T(8,128)(2,1)} %gy_ref.1, f32[32,2,256]{2,1,0:T(2,128)} %pad_maximum_fusion.tab_ref, f32[32,1,256]{2,1,0:T(1,128)} %get-tuple-element.13.own_ref, bf16[4096,1024]{1,0:T(8,128)(2,1)} %bitcast.40, ...), custom_call_target="tpu_custom_call" | custom-call | tf_op jit(solution)/shard_map/moe_bwd/pallas_call | solution.py:331
  180.6 0.0 copy-start.2
  180.6 5.1 %fusion = f32[256,1,8]{2,1,0:T(1,128)S(1)} fusion(bf16[256,8,1024]{2,1,0:T(8,128)(2,1)} %param.17, bf16[256,1024,1]{1,0,2:T(8,128)(2,1)} %bitcast.49), kind=kOutput, calls=%fused_computation | convolution fusion | flops 4194304 | bytes 4726784 | tf_op jit(solution)/shard_map/td,tkd->tk/dot_general | solution.py:326
  185.6 0.0 copy-start.1
  185.6 0.7 copy.18
  186.3 0.0 copy-done.2
  186.3 0.8 copy.25
  187.1 0.0 copy-start
  187.1 3.2 %copy.26 = f32[1,1024,512]{2,1,0:T(8,128)} copy(f32[1,1024,512]{2,1,0:T(8,128)} %bitcast.45) | data formatting | bytes 4194304
  190.3 0.0 copy-done.1
  190.3 1.3 copy.27
  191.7 0.0 copy-done
  191.7 1.3 copy.28
Async XLA Ops:
  180.6 5.8 %copy-start.2 = (bf16[256,1024]{1,0:T(8,128)(2,1)S(1)}, bf16[256,1024]{1,0:T(8,128)(2,1)}, u32[]{:S(2)}) copy-start(bf16[256,1024]{1,0:T(8,128)(2,1)} %get-tuple-element.44) | copy-start | bytes 1572868
  185.6 4.7 %copy-start.1 = (f32[1024,512]{1,0:T(8,128)S(1)}, f32[1024,512]{1,0:T(8,128)}, u32[]{:S(2)}) copy-start(f32[1024,512]{1,0:T(8,128)} %get-tuple-element.11) | copy-start | bytes 6291460
  187.1 4.6 %copy-start = (f32[512,1024]{1,0:T(8,128)S(1)}, f32[512,1024]{1,0:T(8,128)}, u32[]{:S(2)}) copy-start(f32[512,1024]{1,0:T(8,128)} %get-tuple-element.12) | copy-start | bytes 6291460

commit v2 on v1

v2 whole, which is shorter than its diff:
```python
import functools
import math

import jax
import jax.numpy as jnp
from jax import lax
from jax.experimental import pallas as pl
from jax.experimental.pallas import tpu as pltpu
from jax.sharding import PartitionSpec as P

MESH = pl.DeviceIdType.MESH
CORES = 2
BF16, F32 = jnp.bfloat16, jnp.float32

ORDER = ((0, 0), (-1, 0), (1, 0), (0, -1), (0, 1), (2, 0), (0, 2), (-1, -1), (1, 1), (-1, 1), (1, -1), (2, -1), (-1, 2), (2, 1), (1, 2), (2, 2))

EVENTS = {
    1: ((-1, 0), (1, 0), (0, -1), (0, 1)),
    3: ((2, 0), (0, 2)),
    5: ((-1, -1), (-1, 1), (1, -1), (1, 1)),
    7: ((2, -1), (2, 1)),
    9: ((-1, 2), (1, 2)),
    10: ((2, 2),),
}
LAG = 3

NN = (((1,), (0,)), ((), ()))
NT = (((1,), (1,)), ((), ()))
TN = (((0,), (0,)), ((), ()))


def dot(a, b, dims):
    return lax.dot_general(a, b, dims, preferred_element_type=F32)


def lut(k, vals):
    out = vals[0]
    for i, v in enumerate(vals):
        if i:
            out = jnp.where(k == i, v, out)
    return out


def kernel(n_dev, side, gy_ref, ids_ref, slots_ref, gates_ref, pc_ref, y_ref, x_ref, hg_ref, hu_ref, wg_ref, wu_ref, wd_ref,
           gx_ref, gg_ref, gwg_ref, gwu_ref, gwd_ref,
           tokens, stab, tabs, mids, mslots, rbuf, ret, relay, part, hop_in, fin, wgu, wd, xb, hgb, hub,
           tok_sem, tab_sem, meta_sem, ret_sem, relay_sem, hop_sem, fin_sem,
           ag_send, pair_send, tab_send, meta_send, ret_send, relay_send, part_send, load_sem, w_sem):
    me = lax.axis_index("ep")
    core = me % CORES
    mx = (me // CORES) % side
    my = me // (CORES * side)
    my_a = (1 - core) * mx + core * my
    my_b = (1 - core) * my + core * mx
    tok_dev, model_dim = gy_ref.shape
    top_k = ids_ref.shape[0]
    ffn = wg_ref.shape[1]
    cap = rbuf.shape[1]
    half = tok_dev // 2
    n_chip = side * side
    crow = CORES * cap
    partner = me + 1 - 2 * core

    def wrap(v):
        return (v + 2 * side) % side

    def device(x, y, c):
        return (wrap(y) * side + wrap(x)) * CORES + c

    def plane(a, b):
        return device(mx + (1 - core) * a + core * b, my + core * a + (1 - core) * b, core)

    def remote(src, dst, send_sem, recv_sem, to):
        return pltpu.make_async_remote_copy(src_ref=src, dst_ref=dst, send_sem=send_sem, recv_sem=recv_sem, device_id={"ep": to}, device_id_type=MESH)

    def landed(ref, sem):
        pltpu.make_async_copy(ref, ref, sem).wait()

    barrier = pltpu.get_barrier_semaphore()

    def signal_one(i, carry):
        pl.semaphore_signal(barrier, inc=1, device_id={"ep": (me + 1 + i) % n_dev}, device_id_type=MESH)
        return carry

    lax.fori_loop(0, n_dev - 1, signal_one, 0)

    wcopies = [
        pltpu.make_async_copy(wd_ref, wd, w_sem.at[0]),
        pltpu.make_async_copy(wg_ref, wgu.at[:, pl.ds(0, ffn)], w_sem.at[1]),
        pltpu.make_async_copy(wu_ref, wgu.at[:, pl.ds(ffn, ffn)], w_sem.at[2]),
    ]
    for c in wcopies:
        c.start()
    own_copies = [
        pltpu.make_async_copy(gy_ref, tokens.at[me], tok_sem.at[me, 0]),
        pltpu.make_async_copy(ids_ref, mids.at[my_b], meta_sem.at[my_b, 0]),
        pltpu.make_async_copy(slots_ref, mslots.at[my_b], meta_sem.at[my_b, 1]),
    ]
    for c in own_copies:
        c.start()

    def offset(k, axis):
        return lut(k, [o[axis] for o in ORDER])

    def chip_at(k):
        return wrap(my + offset(k, 1)) * side + wrap(mx + offset(k, 0))

    def loads(k):
        q = chip_at(k)
        slot = k % 2
        rows = pl.ds(pl.multiple_of(q * crow, crow), crow)
        return [
            pltpu.make_async_copy(x_ref.at[rows], xb.at[slot], load_sem.at[0, slot]),
            pltpu.make_async_copy(hg_ref.at[rows], hgb.at[slot], load_sem.at[1, slot]),
            pltpu.make_async_copy(hu_ref.at[rows], hub.at[slot], load_sem.at[2, slot]),
        ]

    for c in loads(0):
        c.start()

    ids = ids_ref[...]
    slots = slots_ref[...]
    gates = gates_ref[...]

    def table(e, carry):
        hit = ids == e
        slot = jnp.max(jnp.where(hit, slots, -1), axis=0, keepdims=True)
        slot = jnp.where(slot < pc_ref[0, e], slot, -1)
        gate = jnp.sum(jnp.where(hit, gates, 0.0), axis=0, keepdims=True)
        stab[e] = jnp.concatenate([slot.astype(F32), gate], axis=0)
        return carry

    lax.fori_loop(0, n_dev, table, 0)
    gwg_ref[...] = jnp.zeros_like(gwg_ref)
    gwu_ref[...] = jnp.zeros_like(gwu_ref)
    gwd_ref[...] = jnp.zeros_like(gwd_ref)
    pl.semaphore_wait(barrier, n_dev - 1)

    sends, pairs = [], []

    def block(src, part_no):
        if part_no == "full":
            return tokens.at[src]
        return tokens.at[src, pl.ds(part_no * half, half)]

    def forward_msg(n, i, j, part_no, a, b):
        src = plane(i, j)
        ref = gy_ref if i == 0 and j == 0 else block(src, part_no)
        return remote(ref, block(src, part_no), ag_send.at[n], tok_sem.at[src, 1 if part_no == 1 else 0], plane(a, b))

    def forward(*what):
        what = (len(sends), *what)
        sends.append(what)
        forward_msg(*what).start()

    def pair_msg(n, i, j):
        src = plane(i, j)
        ref = gy_ref if i == 0 and j == 0 else tokens.at[src]
        return remote(ref, tokens.at[src], pair_send.at[n], tok_sem.at[src, 0], partner)

    def to_partner(i, j):
        what = (len(pairs), i, j)
        pairs.append(what)
        pair_msg(*what).start()

    def arrived(src, part_no):
        landed(block(src, part_no), tok_sem.at[src, 1 if part_no == 1 else 0])

    to_partner(0, 0)

    def tab_msg(i):
        to = (me + 1 + i) % n_dev
        return remote(stab.at[to], tabs.at[me], tab_send.at[i], tab_sem.at[me], to)

    def tab_start(i, carry):
        tab_msg(i).start()
        return carry

    lax.fori_loop(0, n_dev - 1, tab_start, 0)
    tab_copy = pltpu.make_async_copy(stab.at[me], tabs.at[me], tab_sem.at[me])
    tab_copy.start()
    for a, b in ((1, 0), (-1, 0), (0, 1), (0, -1)):
        forward(0, 0, "full", a, b)

    def meta_msgs():
        out = []
        for n, j in enumerate((1, -1, 2)):
            out.append(remote(ids_ref, mids.at[my_b], meta_send.at[n, 0], meta_sem.at[my_b, 0], plane(0, j)))
            out.append(remote(slots_ref, mslots.at[my_b], meta_send.at[n, 1], meta_sem.at[my_b, 1], plane(0, j)))
        return out

    for c in meta_msgs():
        c.start()
    own_copies[0].wait()

    def event(i, j):
        src = plane(i, j)
        if i == 2 and j == 0 or j == 2:
            arrived(src, 0)
            arrived(src, 1)
        else:
            arrived(src, "full")
        if j == 0:
            if i == -1:
                forward(i, j, 0, 1, 0)
            if i == 1:
                forward(i, j, 1, -1, 0)
            forward(i, j, "full", 0, 1)
            forward(i, j, "full", 0, -1)
        elif j == -1:
            forward(i, j, 0, 0, 1)
        elif j == 1:
            forward(i, j, 1, 0, -1)
        to_partner(i, j)

    def r_block(k, cc):
        i, j = offset(k, cc), offset(k, 1 - cc)
        a, b = (mx, my) if cc == 0 else (my, mx)
        hb = wrap(b + j)
        home = chip_at(k) * CORES + cc
        step = jnp.where(i == 2, 1 - 2 * core, i)
        to = device(mx + step, my, cc) if cc == 0 else device(mx, my + step, cc)
        slot = (hb * side + a) * CORES + core
        hop = hb * 2 + core
        is_local = jnp.logical_and(i == 0, core == cc)
        return i, home, to, slot, hop, is_local

    def send_chunk(k):
        for cc in range(CORES):
            i, home, to, slot, hop, is_local = r_block(k, cc)

            @pl.when(is_local)
            def _():
                pltpu.make_async_copy(rbuf.at[home], ret.at[slot], ret_sem.at[slot]).start()

            @pl.when(i == 2)
            def _():
                remote(rbuf.at[home], relay.at[hop], ret_send.at[home], relay_sem.at[hop], to).start()

            @pl.when(jnp.logical_and(i != 2, jnp.logical_not(is_local)))
            def _():
                remote(rbuf.at[home], ret.at[slot], ret_send.at[home], ret_sem.at[slot], to).start()

    def relay_msg(j, way):
        hb = wrap(my_b + j)
        slot = (hb * side + wrap(my_a - 1 + 2 * way)) * CORES + way
        hop = hb * 2 + way
        return hop, remote(relay.at[hop], ret.at[slot], relay_send.at[hop], ret_sem.at[slot], plane(1 - 2 * way, 0))

    def hand_on(k):
        i = jnp.where(core == 0, offset(k, 0), offset(k, 1))
        j = jnp.where(core == 0, offset(k, 1), offset(k, 0))

        @pl.when(i == 2)
        def _():
            for way in range(2):
                hop, msg = relay_msg(j, way)
                landed(relay.at[hop], relay_sem.at[hop])
                msg.start()

    slot_iota = lax.broadcasted_iota(jnp.int32, (cap, tok_dev), 0)
    slot_iota_f = slot_iota.astype(F32)
    for c in wcopies:
        c.wait()

    def chunk(k, carry):
        for at, evs in EVENTS.items():
            @pl.when(k == at)
            def _(evs=evs):
                for i, j in evs:
                    event(i, j)

        @pl.when(k > 0)
        def _():
            send_chunk(k - 1)

        @pl.when(k >= LAG)
        def _():
            hand_on(k - LAG)

        slot = k % 2
        for c in loads(k):
            c.wait()

        @pl.when(k + 1 < n_chip)
        def _():
            for c in loads(k + 1):
                c.start()

        q = chip_at(k)
        arrived(q * CORES + 1 - core, "full")

        d_parts = []
        for cc in range(CORES):
            home = q * CORES + cc
            landed(tabs.at[home], tab_sem.at[home])
            tab = tabs[home]
            pick = tab[0:1, :] == slot_iota_f
            gate = jnp.sum(jnp.where(pick, tab[1:2, :], 0.0), axis=1, keepdims=True)
            rows = dot(pick.astype(F32).astype(BF16), tokens[home], NN)
            d_parts.append((gate * rows).astype(BF16))
        d = jnp.concatenate(d_parts, axis=0)
        da = dot(d, wd[...], NT).astype(BF16).astype(F32)
        h1 = hgb[slot].astype(F32)
        h3 = hub[slot].astype(F32)
        g = jax.nn.sigmoid(h1)
        s = h1 * g
        act = (s * h3).astype(BF16)
        dh1 = (da * h3 * g * (1.0 + h1 * (1.0 - g))).astype(BF16)
        dh3 = (da * s).astype(BF16)
        dh = jnp.concatenate([dh1, dh3], axis=1)
        r = dot(dh, wgu[...], NT).astype(BF16)
        for cc in range(CORES):
            rbuf[q * CORES + cc] = r[cc * cap:(cc + 1) * cap]
        x = xb[slot]
        gwg_ref[...] += dot(x, dh1, TN)
        gwu_ref[...] += dot(x, dh3, TN)
        gwd_ref[...] += dot(act, d, TN)
        return carry

    lax.fori_loop(0, n_chip, chunk, 0)
    send_chunk(jnp.int32(n_chip - 1))

    n_run = crow // top_k
    n_step = tok_dev // n_run

    def y_load(m):
        return pltpu.make_async_copy(y_ref.at[pl.ds(pl.multiple_of(m * crow, crow), crow)], xb.at[m % 2], load_sem.at[0, m % 2])

    y_load(0).start()
    lane = lax.broadcasted_iota(jnp.int32, (crow, tok_dev), 1)
    token_of = lax.broadcasted_iota(jnp.int32, (crow, tok_dev), 0) // top_k
    gg_ref[...] = jnp.zeros_like(gg_ref)

    def gate_grad(m, carry):
        y_load(m).wait()

        @pl.when(m + 1 < n_step)
        def _():
            y_load(m + 1).start()

        gy = gy_ref[pl.ds(pl.multiple_of(m * n_run, n_run), n_run), :].astype(F32)
        gy = jnp.broadcast_to(gy[:, None, :], (n_run, top_k, model_dim)).reshape(crow, model_dim)
        col = jnp.sum(xb[m % 2].astype(F32) * gy, axis=1, keepdims=True)
        put = jnp.where(lane == token_of + m * n_run, col, 0.0)
        gg_ref[...] += jnp.sum(put.reshape(n_run, top_k, tok_dev), axis=0)
        return carry

    for k in range(n_chip - LAG, n_chip):
        hand_on(jnp.int32(k))

    lax.fori_loop(0, n_step, gate_grad, 0)

    def add_rows(n, carry):
        j = lut(n, (2, 1, -1, 0))
        hb = wrap(my_b + j)
        landed(mids.at[hb], meta_sem.at[hb, 0])
        landed(mslots.at[hb], meta_sem.at[hb, 1])
        h_ids = mids[hb]
        h_slots = mslots[hb]
        picks = []
        for sa in range(side):
            for ce in range(CORES):
                slot = (hb * side + sa) * CORES + ce
                landed(ret.at[slot], ret_sem.at[slot])
                x = (1 - core) * sa + core * my_b
                y = (1 - core) * my_b + core * sa
                row = jnp.max(jnp.where(h_ids == (y * side + x) * CORES + ce, h_slots, -1), axis=0, keepdims=True)
                picks.append((row == slot_iota).astype(F32).astype(BF16))
        pick = jnp.concatenate(picks, axis=0)
        rows = ret[pl.ds(hb * side * CORES, side * CORES)].reshape(side * CORES * cap, model_dim)
        part[n] = dot(pick, rows, TN)

        @pl.when(n == 1)
        def _():
            for c in hop_msgs():
                c.start()

        return carry

    def hop_msgs():
        return [
            remote(part.at[0, pl.ds(0, half)], hop_in.at[0], part_send.at[0], hop_sem.at[0], plane(0, 1)),
            remote(part.at[0, pl.ds(half, half)], hop_in.at[1], part_send.at[1], hop_sem.at[1], plane(0, -1)),
        ]

    def fin_msgs():
        return [
            remote(part.at[1], fin.at[0], part_send.at[2], fin_sem.at[0], plane(0, 1)),
            remote(part.at[2], fin.at[1], part_send.at[3], fin_sem.at[1], plane(0, -1)),
        ]

    lax.fori_loop(0, 3, add_rows, 0)
    landed(hop_in.at[0], hop_sem.at[0])
    part[1, pl.ds(0, half)] += hop_in[0]
    landed(hop_in.at[1], hop_sem.at[1])
    part[2, pl.ds(half, half)] += hop_in[1]
    for what in sends:
        forward_msg(*what).wait_send()
    for what in pairs:
        pair_msg(*what).wait_send()
    fins = fin_msgs()
    fins[0].start()
    fins[1].start()
    lax.fori_loop(3, 4, add_rows, 0)


    def tab_done(i, carry):
        tab_msg(i).wait_send()
        return carry

    lax.fori_loop(0, n_dev - 1, tab_done, 0)
    for c in meta_msgs() + hop_msgs():
        c.wait_send()

    def ret_done(k, carry):
        for cc in range(CORES):
            i, home, to, slot, hop, is_local = r_block(k, cc)

            @pl.when(jnp.logical_not(is_local))
            def _():
                remote(rbuf.at[home], ret.at[slot], ret_send.at[home], ret_sem.at[slot], to).wait_send()
        return carry

    lax.fori_loop(0, n_chip, ret_done, 0)
    for j in (0, 1, -1, 2):
        for way in range(2):
            relay_msg(j, way)[1].wait_send()
    landed(fin.at[0], fin_sem.at[0])
    landed(fin.at[1], fin_sem.at[1])
    gx_ref[...] = (part[3] + fin[0] + fin[1]).astype(gx_ref.dtype)
    for c in fins:
        c.wait_send()


def solution(mesh):
    n_dev = mesh.shape["ep"]
    side = math.isqrt(n_dev // CORES)
    rows_spec = P(("dp", "ep"), None)
    cube_spec = P(("dp", "ep"), None, None)
    weight_spec = P("ep", None, None)

    def local_step(grad_y, gate_vals, topk_idx, slot_ids, pair_counts, y_routed, x_disp, h_gate, h_up, w_gate, w_up, w_down):
        assert w_gate.shape[0] == 1
        assert side * side * CORES == n_dev and len(ORDER) == side * side
        cap = x_disp.shape[1] // n_dev
        tok_dev, model_dim = grad_y.shape
        ffn = w_gate.shape[2]
        crow = CORES * cap
        n_chip = side * side
        top_k = topk_idx.shape[1]
        vmem = pl.BlockSpec(memory_space=pltpu.VMEM)
        smem = pl.BlockSpec(memory_space=pltpu.SMEM)
        anym = pl.BlockSpec(memory_space=pl.ANY)
        dma = pltpu.SemaphoreType.DMA
        gx, gg, gwg, gwu, gwd = pl.pallas_call(
            functools.partial(kernel, n_dev, side),
            out_shape=(
                jax.ShapeDtypeStruct((tok_dev, model_dim), BF16),
                jax.ShapeDtypeStruct((top_k, tok_dev), F32),
                jax.ShapeDtypeStruct((model_dim, ffn), F32),
                jax.ShapeDtypeStruct((model_dim, ffn), F32),
                jax.ShapeDtypeStruct((ffn, model_dim), F32),
            ),
            in_specs=[vmem, vmem, vmem, vmem, smem] + [anym] * 7,
            out_specs=(vmem,) * 5,
            scratch_shapes=[
                pltpu.VMEM((n_dev, tok_dev, model_dim), BF16),
                pltpu.VMEM((n_dev, 2, tok_dev), F32),
                pltpu.VMEM((n_dev, 2, tok_dev), F32),
                pltpu.VMEM((side, top_k, tok_dev), jnp.int32),
                pltpu.VMEM((side, top_k, tok_dev), jnp.int32),
                pltpu.VMEM((n_dev, cap, model_dim), BF16),
                pltpu.VMEM((n_dev, cap, model_dim), BF16),
                pltpu.VMEM((2 * side, cap, model_dim), BF16),
                pltpu.VMEM((4, tok_dev, model_dim), F32),
                pltpu.VMEM((2, tok_dev // 2, model_dim), F32),
                pltpu.VMEM((2, tok_dev, model_dim), F32),
                pltpu.VMEM((model_dim, 2 * ffn), BF16),
                pltpu.VMEM((ffn, model_dim), BF16),
                pltpu.VMEM((2, crow, model_dim), BF16),
                pltpu.VMEM((2, crow, ffn), BF16),
                pltpu.VMEM((2, crow, ffn), BF16),
                dma((n_dev, 2)),
                dma((n_dev,)),
                dma((side, 2)),
                dma((n_dev,)),
                dma((2 * side,)),
                dma((2,)),
                dma((2,)),
                dma((32,)),
                dma((n_chip,)),
                dma((n_dev,)),
                dma((3, 2)),
                dma((n_dev,)),
                dma((2 * side,)),
                dma((4,)),
                dma((3, 2)),
                dma((3,)),
            ],
            compiler_params=pltpu.CompilerParams(collective_id=0, has_side_effects=True, vmem_limit_bytes=67043328),
            name="moe_bwd",
        )(grad_y, topk_idx.T, slot_ids.T, gate_vals.T, pair_counts, y_routed.reshape(tok_dev * top_k, model_dim), x_disp[0], h_gate[0], h_up[0], w_gate[0], w_up[0], w_down[0])
        return gx, gg.T, gwg[None], gwu[None], gwd[None]

    return jax.shard_map(local_step, mesh=mesh, in_specs=(rows_spec, rows_spec, rows_spec, rows_spec, rows_spec, cube_spec, cube_spec, cube_spec, cube_spec, weight_spec, weight_spec, weight_spec), out_specs=(rows_spec, rows_spec, cube_spec, cube_spec, cube_spec), check_vma=False)
```

time: 193 us -> 148 us (0.77)
  Pallas kernels: 175 us -> 137 us
  matrix products: 5.06 us -> 0 us
  other arithmetic: 2.36 us -> 0 us
    pallas_call x1, Pallas kernels: 175 us -> 137 us  [local_step(): pl.pallas_call(functools.partial(kernel, n_dev, side), out_shape=(jax.Sha...]
    dot_general x1 -> x0, matrix products: 5.06 us -> none  [local_step(): jnp.einsum('td,tkd->tk', grad_y, y_routed, preferred_element_type=F32)]
    unnamed x10 -> x9, local copies, waits for them, and re-layouts: 6.67 us -> 10.1 us
    slice x3 -> x0, local copies, waits for them, and re-layouts: 3 us -> none  [the longest x1 1 us: routing_tables(): slot_of = jnp.where(hit, slots[j][None, :], slot_of)]
where the time goes in v2:
time: 148 us
  Pallas kernels  137 us (93%)
  local copies, waits for them, and re-layouts  10.1 us (7%)
    pallas_call x1, Pallas kernels, local_step(): pl.pallas_call(functools.partial(kernel, n_dev, side), out_shape=(jax.Sha...  137 us
    unnamed x9, local copies, waits for them, and re-layouts  10.1 us

profile of v2, /device:TPU:97, one launch (start us, length us, event | category | flops | bytes accessed | tf_op | source)
XLA Modules:
  0.0 147.8 jit_solution(17786818850288911349)
XLA Ops:
  0.6 137.1 %moe_bwd.1 = (bf16[256,1024]{1,0:T(8,128)(2,1)}, f32[8,256]{1,0:T(8,128)}, f32[1024,512]{1,0:T(8,128)}, f32[1024,512]{1,0:T(8,128)}, f32[512,1024]{1,0:T(8,128)}) custom-call(bf16[256,1024]{1,0:T(8,128)(2,1)} %gy_ref.1, s32[8,256]{1,0:T(8,128)} %bitcast.24, s32[8,256]{1,0:T(8,128)} %bitcast.25, f32[8,256]{1,0:T(8,128)} %bitcast.26, s32[1,32]{1,0:T(1,128)} %pc_ref.1, ...), custom_call_target="tpu_custom_call" | custom-call | tf_op jit(solution)/shard_map/moe_bwd/pallas_call | solution.py:456
  137.7 1.9 %copy.22 = bf16[256,1024]{1,0:T(8,128)(2,1)} copy(bf16[256,1024]{1,0:T(8,128)(2,1)} %get-tuple-element.20) | data formatting | bytes 1048576
  139.6 1.3 copy.23
  140.9 0.0 copy-start.1
  140.9 3.2 %copy.24 = f32[1,1024,512]{2,1,0:T(8,128)} copy(f32[1,1024,512]{2,1,0:T(8,128)} %bitcast.20) | data formatting | bytes 4194304
  144.1 0.0 copy-done.1
  144.1 0.0 copy-start
  144.1 1.3 copy.25
  145.4 1.0 copy-done
  146.5 1.3 copy.26
Async XLA Ops:
  140.9 3.2 %copy-start.1 = (f32[1024,512]{1,0:T(8,128)S(1)}, f32[1024,512]{1,0:T(8,128)}, u32[]{:S(2)}) copy-start(f32[1024,512]{1,0:T(8,128)} %get-tuple-element.13) | copy-start | bytes 6291460
  144.1 2.3 %copy-start = (f32[512,1024]{1,0:T(8,128)S(1)}, f32[512,1024]{1,0:T(8,128)}, u32[]{:S(2)}) copy-start(f32[512,1024]{1,0:T(8,128)} %get-tuple-element.14) | copy-start | bytes 6291460

commit v3 on v2

--- a/solution.py
+++ b/solution.py
@@ -456,11 +456,11 @@
         gx, gg, gwg, gwu, gwd = pl.pallas_call(
             functools.partial(kernel, n_dev, side),
             out_shape=(
-                jax.ShapeDtypeStruct((tok_dev, model_dim), BF16),
-                jax.ShapeDtypeStruct((top_k, tok_dev), F32),
-                jax.ShapeDtypeStruct((model_dim, ffn), F32),
-                jax.ShapeDtypeStruct((model_dim, ffn), F32),
-                jax.ShapeDtypeStruct((ffn, model_dim), F32),
+                pltpu.VMEM((tok_dev, model_dim), BF16),
+                pltpu.VMEM((top_k, tok_dev), F32),
+                pltpu.VMEM((model_dim, ffn), F32),
+                pltpu.VMEM((model_dim, ffn), F32),
+                pltpu.VMEM((ffn, model_dim), F32),
             ),
             in_specs=[vmem, vmem, vmem, vmem, smem] + [anym] * 7,
             out_specs=(vmem,) * 5,
@@ -498,7 +498,7 @@
                 dma((3, 2)),
                 dma((3,)),
             ],
-            compiler_params=pltpu.CompilerParams(collective_id=0, has_side_effects=True, vmem_limit_bytes=67043328),
+            compiler_params=pltpu.CompilerParams(collective_id=0, has_side_effects=True, vmem_limit_bytes=58720256),
             name="moe_bwd",
         )(grad_y, topk_idx.T, slot_ids.T, gate_vals.T, pair_counts, y_routed.reshape(tok_dev * top_k, model_dim), x_disp[0], h_gate[0], h_up[0], w_gate[0], w_up[0], w_down[0])
         return gx, gg.T, gwg[None], gwu[None], gwd[None]

time: 148 us -> 141 us (0.953)
  local copies, waits for them, and re-layouts: 10.1 us -> 5.35 us
  Pallas kernels: 137 us -> 134 us
    unnamed x9 -> x5, local copies, waits for them, and re-layouts: 10.1 us -> 5.35 us
    pallas_call x1, Pallas kernels: 137 us -> 134 us  [local_step(): pl.pallas_call(functools.partial(kernel, n_dev, side), out_shape=(pltpu.V...]
where the time goes in v3:
time: 141 us; the launch traced here: 140 us
  Pallas kernels  134 us (95%)
  local copies, waits for them, and re-layouts  5.35 us (4%)
    pallas_call x1, Pallas kernels, local_step(): pl.pallas_call(functools.partial(kernel, n_dev, side), out_shape=(pltpu.V...  134 us
    unnamed x5, local copies, waits for them, and re-layouts  5.35 us

profile of v3, /device:TPU:97, one launch (start us, length us, event | category | flops | bytes accessed | tf_op | source)
XLA Modules:
  0.0 140.4 jit_solution(14348987217647304114)
XLA Ops:
  0.6 134.4 %moe_bwd.1 = (bf16[256,1024]{1,0:T(8,128)(2,1)S(1)}, f32[8,256]{1,0:T(8,128)S(1)}, f32[1024,512]{1,0:T(8,128)S(1)}, f32[1024,512]{1,0:T(8,128)S(1)}, f32[512,1024]{1,0:T(8,128)S(1)}) custom-call(bf16[256,1024]{1,0:T(8,128)(2,1)} %gy_ref.1, s32[8,256]{1,0:T(8,128)} %bitcast.25, s32[8,256]{1,0:T(8,128)} %bitcast.26, f32[8,256]{1,0:T(8,128)} %bitcast.27, ...), custom_call_target="tpu_custom_call" | custom-call | tf_op jit(solution)/shard_map/moe_bwd/pallas_call | solution.py:456
  135.0 0.8 copy.22
  135.8 0.6 copy.23
  136.4 1.3 copy.24
  137.7 1.3 copy.25
  139.0 1.3 copy.26

commit v4 on v3

--- a/solution.py
+++ b/solution.py
@@ -12,17 +12,23 @@
 CORES = 2
 BF16, F32 = jnp.bfloat16, jnp.float32
 
-ORDER = ((0, 0), (-1, 0), (1, 0), (0, -1), (0, 1), (2, 0), (0, 2), (-1, -1), (1, 1), (-1, 1), (1, -1), (2, -1), (-1, 2), (2, 1), (1, 2), (2, 2))
-
+ORDER = ((0, 1), (0, 0), (1, 0), (0, -1), (-1, 0), (2, 0), (0, 2), (1, -1), (-1, 1), (-1, -1), (1, 1), (2, 2), (-1, 2), (1, 2), (2, -1), (2, 1))
 EVENTS = {
-    1: ((-1, 0), (1, 0), (0, -1), (0, 1)),
-    3: ((2, 0), (0, 2)),
-    5: ((-1, -1), (-1, 1), (1, -1), (1, 1)),
-    7: ((2, -1), (2, 1)),
-    9: ((-1, 2), (1, 2)),
-    10: ((2, 2),),
+    0: ((0, -1), (1, 0), (0, 1), (-1, 0)),
+    2: ((2, 0),),
+    3: ((1, -1),),
+    5: ((0, 2),),
+    6: ((-1, 1),),
+    7: ((2, -1), (2, 1), (1, 1)),
+    8: ((-1, -1),),
+    11: ((2, 2),),
+    12: ((-1, 2),),
+    13: ((1, 2),),
 }
-LAG = 3
+LAG = 6
+
+LINES = (2, -1, 1, 0)
+PART = {2: 0, 1: 1, -1: 2, 0: 3}
 
 NN = (((1,), (0,)), ((), ()))
 NT = (((1,), (1,)), ((), ()))
@@ -135,18 +141,16 @@
     gwu_ref[...] = jnp.zeros_like(gwu_ref)
     gwd_ref[...] = jnp.zeros_like(gwd_ref)
     pl.semaphore_wait(barrier, n_dev - 1)
+    own_copies[0].wait()
 
     sends, pairs = [], []
 
-    def block(src, part_no):
-        if part_no == "full":
-            return tokens.at[src]
-        return tokens.at[src, pl.ds(part_no * half, half)]
-
-    def forward_msg(n, i, j, part_no, a, b):
+    def block(src, h):
+        return tokens.at[src, pl.ds(h * half, half)]
+
+    def forward_msg(n, i, j, h, a, b):
         src = plane(i, j)
-        ref = gy_ref if i == 0 and j == 0 else block(src, part_no)
-        return remote(ref, block(src, part_no), ag_send.at[n], tok_sem.at[src, 1 if part_no == 1 else 0], plane(a, b))
+        return remote(block(src, h), block(src, h), ag_send.at[n], tok_sem.at[src, h], plane(a, b))
 
     def forward(*what):
         what = (len(sends), *what)
@@ -155,16 +159,15 @@
 
     def pair_msg(n, i, j):
         src = plane(i, j)
-        ref = gy_ref if i == 0 and j == 0 else tokens.at[src]
-        return remote(ref, tokens.at[src], pair_send.at[n], tok_sem.at[src, 0], partner)
+        return remote(tokens.at[src], tokens.at[src], pair_send.at[n], tok_sem.at[src, 0], partner)
 
     def to_partner(i, j):
         what = (len(pairs), i, j)
         pairs.append(what)
         pair_msg(*what).start()
 
-    def arrived(src, part_no):
-        landed(block(src, part_no), tok_sem.at[src, 1 if part_no == 1 else 0])
+    def arrived(src, h):
+        landed(block(src, h), tok_sem.at[src, h])
 
     to_partner(0, 0)
 
@@ -179,8 +182,9 @@
     lax.fori_loop(0, n_dev - 1, tab_start, 0)
     tab_copy = pltpu.make_async_copy(stab.at[me], tabs.at[me], tab_sem.at[me])
     tab_copy.start()
-    for a, b in ((1, 0), (-1, 0), (0, 1), (0, -1)):
-        forward(0, 0, "full", a, b)
+    for n in range(2):
+        for a, b, h in ((1, 0, n), (-1, 0, 1 - n), (0, 1, n), (0, -1, 1 - n)):
+            forward(0, 0, h, a, b)
 
     def meta_msgs():
         out = []
@@ -191,26 +195,19 @@
 
     for c in meta_msgs():
         c.start()
-    own_copies[0].wait()
 
     def event(i, j):
         src = plane(i, j)
-        if i == 2 and j == 0 or j == 2:
-            arrived(src, 0)
-            arrived(src, 1)
-        else:
-            arrived(src, "full")
-        if j == 0:
-            if i == -1:
-                forward(i, j, 0, 1, 0)
-            if i == 1:
-                forward(i, j, 1, -1, 0)
-            forward(i, j, "full", 0, 1)
-            forward(i, j, "full", 0, -1)
-        elif j == -1:
-            forward(i, j, 0, 0, 1)
-        elif j == 1:
-            forward(i, j, 1, 0, -1)
+        first = 1 if (i == 1 and j == 0) or j == 1 else 0
+        for n, h in enumerate((first, 1 - first)):
+            arrived(src, h)
+            if j == 0:
+                if n == 0 and abs(i) == 1:
+                    forward(i, j, h, -i, 0)
+                forward(i, j, h, 0, 1)
+                forward(i, j, h, 0, -1)
+            elif n == 0 and abs(j) == 1:
+                forward(i, j, h, 0, -j)
         to_partner(i, j)
 
     def r_block(k, cc):
@@ -288,7 +285,7 @@
                 c.start()
 
         q = chip_at(k)
-        arrived(q * CORES + 1 - core, "full")
+        landed(tokens.at[q * CORES + 1 - core], tok_sem.at[q * CORES + 1 - core, 0])
 
         d_parts = []
         for cc in range(CORES):
@@ -339,7 +336,7 @@
         def _():
             y_load(m + 1).start()
 
-        gy = gy_ref[pl.ds(pl.multiple_of(m * n_run, n_run), n_run), :].astype(F32)
+        gy = tokens[me, pl.ds(pl.multiple_of(m * n_run, n_run), n_run), :].astype(F32)
         gy = jnp.broadcast_to(gy[:, None, :], (n_run, top_k, model_dim)).reshape(crow, model_dim)
         col = jnp.sum(xb[m % 2].astype(F32) * gy, axis=1, keepdims=True)
         put = jnp.where(lane == token_of + m * n_run, col, 0.0)
@@ -349,10 +346,10 @@
     for k in range(n_chip - LAG, n_chip):
         hand_on(jnp.int32(k))
 
-    lax.fori_loop(0, n_step, gate_grad, 0)
+    lax.fori_loop(0, n_step - 1, gate_grad, 0)
 
     def add_rows(n, carry):
-        j = lut(n, (2, 1, -1, 0))
+        j = lut(n, LINES)
         hb = wrap(my_b + j)
         landed(mids.at[hb], meta_sem.at[hb, 0])
         landed(mslots.at[hb], meta_sem.at[hb, 1])
@@ -369,10 +366,11 @@
                 picks.append((row == slot_iota).astype(F32).astype(BF16))
         pick = jnp.concatenate(picks, axis=0)
         rows = ret[pl.ds(hb * side * CORES, side * CORES)].reshape(side * CORES * cap, model_dim)
-        part[n] = dot(pick, rows, TN)
-
-        @pl.when(n == 1)
+        part[lut(n, [PART[v] for v in LINES])] = dot(pick, rows, TN)
+
+        @pl.when(n == 0)
         def _():
+            gate_grad(n_step - 1, 0)
             for c in hop_msgs():
                 c.start()
 
@@ -386,11 +384,15 @@
 
     def fin_msgs():
         return [
-            remote(part.at[1], fin.at[0], part_send.at[2], fin_sem.at[0], plane(0, 1)),
-            remote(part.at[2], fin.at[1], part_send.at[3], fin_sem.at[1], plane(0, -1)),
+            remote(part.at[1 + n, pl.ds(h * half, half)], fin.at[n, pl.ds(h * half, half)], part_send.at[2 + 2 * n + h], fin_sem.at[n, h], plane(0, 1 - 2 * n))
+            for n in range(2)
+            for h in range(2)
         ]
 
-    lax.fori_loop(0, 3, add_rows, 0)
+    fins = fin_msgs()
+    lax.fori_loop(0, len(LINES), add_rows, 0)
+    fins[1].start()
+    fins[2].start()
     landed(hop_in.at[0], hop_sem.at[0])
     part[1, pl.ds(0, half)] += hop_in[0]
     landed(hop_in.at[1], hop_sem.at[1])
@@ -399,10 +401,8 @@
         forward_msg(*what).wait_send()
     for what in pairs:
         pair_msg(*what).wait_send()
-    fins = fin_msgs()
     fins[0].start()
-    fins[1].start()
-    lax.fori_loop(3, 4, add_rows, 0)
+    fins[3].start()
 
 
     def tab_done(i, carry):
@@ -426,11 +426,22 @@
     for j in (0, 1, -1, 2):
         for way in range(2):
             relay_msg(j, way)[1].wait_send()
-    landed(fin.at[0], fin_sem.at[0])
-    landed(fin.at[1], fin_sem.at[1])
+    for n in range(2):
+        for h in range(2):
+            landed(fin.at[n, pl.ds(h * half, half)], fin_sem.at[n, h])
     gx_ref[...] = (part[3] + fin[0] + fin[1]).astype(gx_ref.dtype)
     for c in fins:
         c.wait_send()
+
+
+def write_out(*refs):
+    n = len(refs) // 2
+    sems = refs[-1]
+    copies = [pltpu.make_async_copy(refs[i], refs[n + i], sems.at[i]) for i in range(n)]
+    for c in copies:
+        c.start()
+    for c in copies:
+        c.wait()
 
 
 def solution(mesh):
@@ -453,7 +464,7 @@
         smem = pl.BlockSpec(memory_space=pltpu.SMEM)
         anym = pl.BlockSpec(memory_space=pl.ANY)
         dma = pltpu.SemaphoreType.DMA
-        gx, gg, gwg, gwu, gwd = pl.pallas_call(
+        results = pl.pallas_call(
             functools.partial(kernel, n_dev, side),
             out_shape=(
                 pltpu.VMEM((tok_dev, model_dim), BF16),
@@ -462,7 +473,7 @@
                 pltpu.VMEM((model_dim, ffn), F32),
                 pltpu.VMEM((ffn, model_dim), F32),
             ),
-            in_specs=[vmem, vmem, vmem, vmem, smem] + [anym] * 7,
+            in_specs=[anym, vmem, vmem, vmem, smem] + [anym] * 7,
             out_specs=(vmem,) * 5,
             scratch_shapes=[
                 pltpu.VMEM((n_dev, tok_dev, model_dim), BF16),
@@ -487,20 +498,29 @@
                 dma((n_dev,)),
                 dma((2 * side,)),
                 dma((2,)),
-                dma((2,)),
-                dma((32,)),
+                dma((2, 2)),
+                dma((64,)),
                 dma((n_chip,)),
                 dma((n_dev,)),
                 dma((3, 2)),
                 dma((n_dev,)),
                 dma((2 * side,)),
-                dma((4,)),
+                dma((6,)),
                 dma((3, 2)),
                 dma((3,)),
             ],
             compiler_params=pltpu.CompilerParams(collective_id=0, has_side_effects=True, vmem_limit_bytes=58720256),
             name="moe_bwd",
         )(grad_y, topk_idx.T, slot_ids.T, gate_vals.T, pair_counts, y_routed.reshape(tok_dev * top_k, model_dim), x_disp[0], h_gate[0], h_up[0], w_gate[0], w_up[0], w_down[0])
+        gx, gg, gwg, gwu, gwd = pl.pallas_call(
+            write_out,
+            out_shape=tuple(jax.ShapeDtypeStruct(r.shape, r.dtype) for r in results),
+            in_specs=[anym] * len(results),
+            out_specs=(anym,) * len(results),
+            scratch_shapes=[dma((len(results),))],
+            compiler_params=pltpu.CompilerParams(vmem_limit_bytes=1048576),
+            name="write_out",
+        )(*results)
         return gx, gg.T, gwg[None], gwu[None], gwd[None]
 
     return jax.shard_map(local_step, mesh=mesh, in_specs=(rows_spec, rows_spec, rows_spec, rows_spec, rows_spec, cube_spec, cube_spec, cube_spec, cube_spec, weight_spec, weight_spec, weight_spec), out_specs=(rows_spec, rows_spec, cube_spec, cube_spec, cube_spec), check_vma=False)

time: 141 us -> 130 us (0.922)
  the two profiles are of different devices: /device:TPU:97 before, /device:TPU:98 now
where the time goes in v4:
time: 130 us
  Pallas kernels  129 us (99%)
    pallas_call x1, Pallas kernels, local_step(): pl.pallas_call(functools.partial(kernel, n_dev, side), out_shape=(pltpu.V...  126 us
    pallas_call x1, Pallas kernels, local_step(): pl.pallas_call(write_out, out_shape=tuple((jax.ShapeDtypeStruct(r.shape,...  2.92 us

profile of v4, /device:TPU:98, one launch (start us, length us, event | category | flops | bytes accessed | tf_op | source)
XLA Modules:
  0.0 130.0 jit_solution(10968526276129599155)
XLA Ops:
  0.6 126.4 %moe_bwd.1 = (bf16[256,1024]{1,0:T(8,128)(2,1)S(1)}, f32[8,256]{1,0:T(8,128)S(1)}, f32[1024,512]{1,0:T(8,128)S(1)}, f32[1024,512]{1,0:T(8,128)S(1)}, f32[512,1024]{1,0:T(8,128)S(1)}) custom-call(bf16[256,1024]{1,0:T(8,128)(2,1)} %gy_ref.1, s32[8,256]{1,0:T(8,128)} %bitcast.21, s32[8,256]{1,0:T(8,128)} %bitcast.22, f32[8,256]{1,0:T(8,128)} %bitcast.23, ...), custom_call_target="tpu_custom_call" | custom-call | tf_op jit(solution)/shard_map/moe_bwd/pallas_call | solution.py:467
  127.0 2.9 %write_out.1 = (bf16[256,1024]{1,0:T(8,128)(2,1)}, f32[8,256]{1,0:T(8,128)}, f32[1024,512]{1,0:T(8,128)}, f32[1024,512]{1,0:T(8,128)}, f32[512,1024]{1,0:T(8,128)}) custom-call(bf16[256,1024]{1,0:T(8,128)(2,1)S(1)} %get-tuple-element.15.refs_0_, f32[8,256]{1,0:T(8,128)S(1)} %get-tuple-element.16.refs_1_, f32[1024,512]{1,0:T(8,128)S(1)} %get-tuple-element.17.refs_2_, ...), custom_call_target="tpu_custom_call" | custom-call | tf_op jit(solution)/shard_map/write_out/pallas_call | solution.py:515

commit v5 on v4

--- a/solution.py
+++ b/solution.py
@@ -12,7 +12,7 @@
 CORES = 2
 BF16, F32 = jnp.bfloat16, jnp.float32
 
-ORDER = ((0, 1), (0, 0), (1, 0), (0, -1), (-1, 0), (2, 0), (0, 2), (1, -1), (-1, 1), (-1, -1), (1, 1), (2, 2), (-1, 2), (1, 2), (2, -1), (2, 1))
+ORDER = ((1, 0), (0, 0), (0, 1), (-1, 0), (0, -1), (0, 2), (2, 0), (-1, 1), (1, -1), (-1, -1), (1, 1), (2, 2), (2, -1), (2, 1), (-1, 2), (1, 2))
 EVENTS = {
     0: ((0, -1), (1, 0), (0, 1), (-1, 0)),
     2: ((2, 0),),
@@ -25,6 +25,7 @@
     12: ((-1, 2),),
     13: ((1, 2),),
 }
+FLIP = 1
 LAG = 6
 
 LINES = (2, -1, 1, 0)
@@ -56,8 +57,9 @@
     core = me % CORES
     mx = (me // CORES) % side
     my = me // (CORES * side)
-    my_a = (1 - core) * mx + core * my
-    my_b = (1 - core) * my + core * mx
+    turn = 1 - core if FLIP else core
+    my_a = (1 - turn) * mx + turn * my
+    my_b = (1 - turn) * my + turn * mx
     tok_dev, model_dim = gy_ref.shape
     top_k = ids_ref.shape[0]
     ffn = wg_ref.shape[1]
@@ -74,7 +76,7 @@
         return (wrap(y) * side + wrap(x)) * CORES + c
 
     def plane(a, b):
-        return device(mx + (1 - core) * a + core * b, my + core * a + (1 - core) * b, core)
+        return device(mx + (1 - turn) * a + turn * b, my + turn * a + (1 - turn) * b, core)
 
     def remote(src, dst, send_sem, recv_sem, to):
         return pltpu.make_async_remote_copy(src_ref=src, dst_ref=dst, send_sem=send_sem, recv_sem=recv_sem, device_id={"ep": to}, device_id_type=MESH)
@@ -211,12 +213,13 @@
         to_partner(i, j)
 
     def r_block(k, cc):
-        i, j = offset(k, cc), offset(k, 1 - cc)
-        a, b = (mx, my) if cc == 0 else (my, mx)
+        axis = 1 - cc if FLIP else cc
+        i, j = offset(k, axis), offset(k, 1 - axis)
+        a, b = (mx, my) if axis == 0 else (my, mx)
         hb = wrap(b + j)
         home = chip_at(k) * CORES + cc
         step = jnp.where(i == 2, 1 - 2 * core, i)
-        to = device(mx + step, my, cc) if cc == 0 else device(mx, my + step, cc)
+        to = device(mx + step, my, cc) if axis == 0 else device(mx, my + step, cc)
         slot = (hb * side + a) * CORES + core
         hop = hb * 2 + core
         is_local = jnp.logical_and(i == 0, core == cc)
@@ -245,8 +248,8 @@
         return hop, remote(relay.at[hop], ret.at[slot], relay_send.at[hop], ret_sem.at[slot], plane(1 - 2 * way, 0))
 
     def hand_on(k):
-        i = jnp.where(core == 0, offset(k, 0), offset(k, 1))
-        j = jnp.where(core == 0, offset(k, 1), offset(k, 0))
+        i = jnp.where(turn == 0, offset(k, 0), offset(k, 1))
+        j = jnp.where(turn == 0, offset(k, 1), offset(k, 0))
 
         @pl.when(i == 2)
         def _():
@@ -360,8 +363,8 @@
             for ce in range(CORES):
                 slot = (hb * side + sa) * CORES + ce
                 landed(ret.at[slot], ret_sem.at[slot])
-                x = (1 - core) * sa + core * my_b
-                y = (1 - core) * my_b + core * sa
+                x = (1 - turn) * sa + turn * my_b
+                y = (1 - turn) * my_b + turn * sa
                 row = jnp.max(jnp.where(h_ids == (y * side + x) * CORES + ce, h_slots, -1), axis=0, keepdims=True)
                 picks.append((row == slot_iota).astype(F32).astype(BF16))
         pick = jnp.concatenate(picks, axis=0)

time: 130 us -> 129 us (level)
  the two profiles are of different devices: /device:TPU:98 before, /device:TPU:104 now
where the time goes in v5:
time: 129 us
  Pallas kernels  128 us (99%)
    pallas_call x1, Pallas kernels, local_step(): pl.pallas_call(functools.partial(kernel, n_dev, side), out_shape=(pltpu.V...  125 us
    pallas_call x1, Pallas kernels, local_step(): pl.pallas_call(write_out, out_shape=tuple((jax.ShapeDtypeStruct(r.shape,...  2.92 us

profile of v5, /device:TPU:104, one launch (start us, length us, event | category | flops | bytes accessed | tf_op | source)
XLA Modules:
  0.0 128.8 jit_solution(8218450695203467271)
XLA Ops:
  0.6 125.2 %moe_bwd.1 = (bf16[256,1024]{1,0:T(8,128)(2,1)S(1)}, f32[8,256]{1,0:T(8,128)S(1)}, f32[1024,512]{1,0:T(8,128)S(1)}, f32[1024,512]{1,0:T(8,128)S(1)}, f32[512,1024]{1,0:T(8,128)S(1)}) custom-call(bf16[256,1024]{1,0:T(8,128)(2,1)} %gy_ref.1, s32[8,256]{1,0:T(8,128)} %bitcast.21, s32[8,256]{1,0:T(8,128)} %bitcast.22, f32[8,256]{1,0:T(8,128)} %bitcast.23, ...), custom_call_target="tpu_custom_call" | custom-call | tf_op jit(solution)/shard_map/moe_bwd/pallas_call | solution.py:470
  125.9 2.9 %write_out.1 = (bf16[256,1024]{1,0:T(8,128)(2,1)}, f32[8,256]{1,0:T(8,128)}, f32[1024,512]{1,0:T(8,128)}, f32[1024,512]{1,0:T(8,128)}, f32[512,1024]{1,0:T(8,128)}) custom-call(bf16[256,1024]{1,0:T(8,128)(2,1)S(1)} %get-tuple-element.15.refs_0_, f32[8,256]{1,0:T(8,128)S(1)} %get-tuple-element.16.refs_1_, f32[1024,512]{1,0:T(8,128)S(1)} %get-tuple-element.17.refs_2_, ...), custom_call_target="tpu_custom_call" | custom-call | tf_op jit(solution)/shard_map/write_out/pallas_call | solution.py:518

commit v6 on v5

--- a/solution.py
+++ b/solution.py
@@ -12,23 +12,22 @@
 CORES = 2
 BF16, F32 = jnp.bfloat16, jnp.float32
 
-ORDER = ((1, 0), (0, 0), (0, 1), (-1, 0), (0, -1), (0, 2), (2, 0), (-1, 1), (1, -1), (-1, -1), (1, 1), (2, 2), (2, -1), (2, 1), (-1, 2), (1, 2))
+ORDER = ((-1, 0), (0, 1), (0, -1), (0, 0), (-1, 1), (1, 0), (1, -1), (1, 1), (0, 2), (-1, -1), (2, 0), (2, 1), (2, -1), (2, 2), (1, 2), (-1, 2))
 EVENTS = {
-    0: ((0, -1), (1, 0), (0, 1), (-1, 0)),
-    2: ((2, 0),),
-    3: ((1, -1),),
-    5: ((0, 2),),
-    6: ((-1, 1),),
-    7: ((2, -1), (2, 1), (1, 1)),
-    8: ((-1, -1),),
-    11: ((2, 2),),
-    12: ((-1, 2),),
-    13: ((1, 2),),
+    0: ((-1, 0), (0, -1), (1, 0), (0, 1)),
+    2: ((2, 0), (-1, 1)),
+    4: ((0, 2), (1, -1), (-1, -1)),
+    5: ((1, 1),),
+    6: ((2, -1),),
+    9: ((2, 1),),
+    10: ((1, 2),),
+    12: ((2, 2), (-1, 2)),
 }
 FLIP = 1
-LAG = 6
-
-LINES = (2, -1, 1, 0)
+RELAY = {15: (11,)}
+TAIL_RELAY = (13, 10, 8, 14), (15, 12)
+
+LINES = (2, 0, -1, 1)
 PART = {2: 0, 1: 1, -1: 2, 0: 3}
 
 NN = (((1,), (0,)), ((), ()))
@@ -248,8 +247,9 @@
         return hop, remote(relay.at[hop], ret.at[slot], relay_send.at[hop], ret_sem.at[slot], plane(1 - 2 * way, 0))
 
     def hand_on(k):
-        i = jnp.where(turn == 0, offset(k, 0), offset(k, 1))
-        j = jnp.where(turn == 0, offset(k, 1), offset(k, 0))
+        dx, dy = ORDER[k]
+        i = jnp.where(turn == 0, dx, dy)
+        j = jnp.where(turn == 0, dy, dx)
 
         @pl.when(i == 2)
         def _():
@@ -274,9 +274,11 @@
         def _():
             send_chunk(k - 1)
 
-        @pl.when(k >= LAG)
-        def _():
-            hand_on(k - LAG)
+        for at, steps in RELAY.items():
+            @pl.when(k == at)
+            def _(steps=steps):
+                for n in steps:
+                    hand_on(n)
 
         slot = k % 2
         for c in loads(k):
@@ -346,10 +348,11 @@
         gg_ref[...] += jnp.sum(put.reshape(n_run, top_k, tok_dev), axis=0)
         return carry
 
-    for k in range(n_chip - LAG, n_chip):
-        hand_on(jnp.int32(k))
-
-    lax.fori_loop(0, n_step - 1, gate_grad, 0)
+    for k in TAIL_RELAY[0]:
+        hand_on(k)
+    lax.fori_loop(0, n_step, gate_grad, 0)
+    for k in TAIL_RELAY[1]:
+        hand_on(k)
 
     def add_rows(n, carry):
         j = lut(n, LINES)
@@ -371,9 +374,8 @@
         rows = ret[pl.ds(hb * side * CORES, side * CORES)].reshape(side * CORES * cap, model_dim)
         part[lut(n, [PART[v] for v in LINES])] = dot(pick, rows, TN)
 
-        @pl.when(n == 0)
+        @pl.when(n == 1)
         def _():
-            gate_grad(n_step - 1, 0)
             for c in hop_msgs():
                 c.start()
 
@@ -394,25 +396,24 @@
 
     fins = fin_msgs()
     lax.fori_loop(0, len(LINES), add_rows, 0)
+    fins[2].start()
+    for what in sends:
+        forward_msg(*what).wait_send()
+    for what in pairs:
+        pair_msg(*what).wait_send()
     fins[1].start()
-    fins[2].start()
     landed(hop_in.at[0], hop_sem.at[0])
     part[1, pl.ds(0, half)] += hop_in[0]
     landed(hop_in.at[1], hop_sem.at[1])
     part[2, pl.ds(half, half)] += hop_in[1]
-    for what in sends:
-        forward_msg(*what).wait_send()
-    for what in pairs:
-        pair_msg(*what).wait_send()
+
+    def tab_done(i, carry):
+        tab_msg(i).wait_send()
+        return carry
+
+    lax.fori_loop(0, n_dev - 1, tab_done, 0)
     fins[0].start()
     fins[3].start()
-
-
-    def tab_done(i, carry):
-        tab_msg(i).wait_send()
-        return carry
-
-    lax.fori_loop(0, n_dev - 1, tab_done, 0)
     for c in meta_msgs() + hop_msgs():
         c.wait_send()
 

time: 129 us -> 126 us (0.977)
  the two profiles are of different devices: /device:TPU:104 before, /device:TPU:97 now
where the time goes in v6:
time: 126 us; the launch traced here: 125 us
  Pallas kernels  125 us (99%)
    pallas_call x1, Pallas kernels, local_step(): pl.pallas_call(functools.partial(kernel, n_dev, side), out_shape=(pltpu.V...  122 us
    pallas_call x1, Pallas kernels, local_step(): pl.pallas_call(write_out, out_shape=tuple((jax.ShapeDtypeStruct(r.shape,...  2.92 us

profile of v6, /device:TPU:97, one launch (start us, length us, event | category | flops | bytes accessed | tf_op | source)
XLA Modules:
  0.0 125.3 jit_solution(6164245752519232520)
XLA Ops:
  0.6 121.7 %moe_bwd.1 = (bf16[256,1024]{1,0:T(8,128)(2,1)S(1)}, f32[8,256]{1,0:T(8,128)S(1)}, f32[1024,512]{1,0:T(8,128)S(1)}, f32[1024,512]{1,0:T(8,128)S(1)}, f32[512,1024]{1,0:T(8,128)S(1)}) custom-call(bf16[256,1024]{1,0:T(8,128)(2,1)} %gy_ref.1, s32[8,256]{1,0:T(8,128)} %bitcast.21, s32[8,256]{1,0:T(8,128)} %bitcast.22, f32[8,256]{1,0:T(8,128)} %bitcast.23, ...), custom_call_target="tpu_custom_call" | custom-call | tf_op jit(solution)/shard_map/moe_bwd/pallas_call | solution.py:471
  122.3 2.9 %write_out.1 = (bf16[256,1024]{1,0:T(8,128)(2,1)}, f32[8,256]{1,0:T(8,128)}, f32[1024,512]{1,0:T(8,128)}, f32[1024,512]{1,0:T(8,128)}, f32[512,1024]{1,0:T(8,128)}) custom-call(bf16[256,1024]{1,0:T(8,128)(2,1)S(1)} %get-tuple-element.15.refs_0_, f32[8,256]{1,0:T(8,128)S(1)} %get-tuple-element.16.refs_1_, f32[1024,512]{1,0:T(8,128)S(1)} %get-tuple-element.17.refs_2_, ...), custom_call_target="tpu_custom_call" | custom-call | tf_op jit(solution)/shard_map/write_out/pallas_call | solution.py:519

commit v7 on v6

--- a/solution.py
+++ b/solution.py
@@ -27,6 +27,7 @@
 RELAY = {15: (11,)}
 TAIL_RELAY = (13, 10, 8, 14), (15, 12)
 
+PIECE = 512 * 1024
 LINES = (2, 0, -1, 1)
 PART = {2: 0, 1: 1, -1: 2, 0: 3}
 
@@ -51,7 +52,7 @@
            gx_ref, gg_ref, gwg_ref, gwu_ref, gwd_ref,
            tokens, stab, tabs, mids, mslots, rbuf, ret, relay, part, hop_in, fin, wgu, wd, xb, hgb, hub,
            tok_sem, tab_sem, meta_sem, ret_sem, relay_sem, hop_sem, fin_sem,
-           ag_send, pair_send, tab_send, meta_send, ret_send, relay_send, part_send, load_sem, w_sem):
+           ag_send, pair_send, tab_send, meta_send, ret_send, relay_send, part_send, load_sem, w_sem, round_sem):
     me = lax.axis_index("ep")
     core = me % CORES
     mx = (me // CORES) % side
@@ -83,13 +84,14 @@
     def landed(ref, sem):
         pltpu.make_async_copy(ref, ref, sem).wait()
 
+    peers = [partner] + [device(mx + dx, my + dy, c) for dx, dy in ((1, 0), (-1, 0), (0, 1), (0, -1)) for c in range(CORES)]
+
+    def tell(sem):
+        for to in peers:
+            pl.semaphore_signal(sem, inc=1, device_id={"ep": to}, device_id_type=MESH)
+
     barrier = pltpu.get_barrier_semaphore()
-
-    def signal_one(i, carry):
-        pl.semaphore_signal(barrier, inc=1, device_id={"ep": (me + 1 + i) % n_dev}, device_id_type=MESH)
-        return carry
-
-    lax.fori_loop(0, n_dev - 1, signal_one, 0)
+    tell(barrier)
 
     wcopies = [
         pltpu.make_async_copy(wd_ref, wd, w_sem.at[0]),
@@ -141,7 +143,7 @@
     gwg_ref[...] = jnp.zeros_like(gwg_ref)
     gwu_ref[...] = jnp.zeros_like(gwu_ref)
     gwd_ref[...] = jnp.zeros_like(gwd_ref)
-    pl.semaphore_wait(barrier, n_dev - 1)
+    pl.semaphore_wait(barrier, len(peers))
     own_copies[0].wait()
 
     sends, pairs = [], []
@@ -180,13 +182,16 @@
         tab_msg(i).start()
         return carry
 
+    for n in range(2):
+        for a, b, h in ((1, 0, n), (-1, 0, 1 - n), (0, 1, n), (0, -1, 1 - n)):
+            forward(0, 0, h, a, b)
+
+    for n in range(side - 1):
+        tell(round_sem.at[n])
+        pl.semaphore_wait(round_sem.at[n], len(peers))
     lax.fori_loop(0, n_dev - 1, tab_start, 0)
     tab_copy = pltpu.make_async_copy(stab.at[me], tabs.at[me], tab_sem.at[me])
     tab_copy.start()
-    for n in range(2):
-        for a, b, h in ((1, 0, n), (-1, 0, 1 - n), (0, 1, n), (0, -1, 1 - n)):
-            forward(0, 0, h, a, b)
-
     def meta_msgs():
         out = []
         for n, j in enumerate((1, -1, 2)):
@@ -430,10 +435,13 @@
     for j in (0, 1, -1, 2):
         for way in range(2):
             relay_msg(j, way)[1].wait_send()
-    for n in range(2):
-        for h in range(2):
-            landed(fin.at[n, pl.ds(h * half, half)], fin_sem.at[n, h])
-    gx_ref[...] = (part[3] + fin[0] + fin[1]).astype(gx_ref.dtype)
+    for n, h in ((0, 1), (1, 0), (0, 0), (1, 1)):
+        rows = pl.ds(h * half, half)
+        landed(fin.at[n, rows], fin_sem.at[n, h])
+        if (n, h) == (0, 0):
+            gx_ref[rows] = (part[3, rows] + fin[0, rows] + fin[1, rows]).astype(gx_ref.dtype)
+    rows = pl.ds(half, half)
+    gx_ref[rows] = (part[3, rows] + fin[0, rows] + fin[1, rows]).astype(gx_ref.dtype)
     for c in fins:
         c.wait_send()
 
@@ -441,7 +449,13 @@
 def write_out(*refs):
     n = len(refs) // 2
     sems = refs[-1]
-    copies = [pltpu.make_async_copy(refs[i], refs[n + i], sems.at[i]) for i in range(n)]
+    copies = []
+    for i in range(n):
+        src, dst = refs[i], refs[n + i]
+        rows = src.shape[0]
+        step = max(8, min(rows, PIECE // (src.shape[1] * src.dtype.itemsize)))
+        for r in range(0, rows, step):
+            copies.append(pltpu.make_async_copy(src.at[pl.ds(r, step)], dst.at[pl.ds(r, step)], sems.at[len(copies)]))
     for c in copies:
         c.start()
     for c in copies:
@@ -512,6 +526,7 @@
                 dma((6,)),
                 dma((3, 2)),
                 dma((3,)),
+                pltpu.SemaphoreType.REGULAR((side - 1,)),
             ],
             compiler_params=pltpu.CompilerParams(collective_id=0, has_side_effects=True, vmem_limit_bytes=58720256),
             name="moe_bwd",
@@ -521,7 +536,7 @@
             out_shape=tuple(jax.ShapeDtypeStruct(r.shape, r.dtype) for r in results),
             in_specs=[anym] * len(results),
             out_specs=(anym,) * len(results),
-            scratch_shapes=[dma((len(results),))],
+            scratch_shapes=[dma((32,))],
             compiler_params=pltpu.CompilerParams(vmem_limit_bytes=1048576),
             name="write_out",
         )(*results)

time: 126 us -> 125 us (level)
  no operation moved by 1% of the time
where the time goes in v7:
time: 125 us
  Pallas kernels  124 us (99%)
    pallas_call x1, Pallas kernels, local_step(): pl.pallas_call(functools.partial(kernel, n_dev, side), out_shape=(pltpu.V...  121 us
    pallas_call x1, Pallas kernels, local_step(): pl.pallas_call(write_out, out_shape=tuple((jax.ShapeDtypeStruct(r.shape,...  3.09 us

profile of v7, /device:TPU:97, one launch (start us, length us, event | category | flops | bytes accessed | tf_op | source)
XLA Modules:
  0.0 124.9 jit_solution(5304886680124420587)
XLA Ops:
  0.6 121.2 %moe_bwd.1 = (bf16[256,1024]{1,0:T(8,128)(2,1)S(1)}, f32[8,256]{1,0:T(8,128)S(1)}, f32[1024,512]{1,0:T(8,128)S(1)}, f32[1024,512]{1,0:T(8,128)S(1)}, f32[512,1024]{1,0:T(8,128)S(1)}) custom-call(bf16[256,1024]{1,0:T(8,128)(2,1)} %gy_ref.1, s32[8,256]{1,0:T(8,128)} %bitcast.21, s32[8,256]{1,0:T(8,128)} %bitcast.22, f32[8,256]{1,0:T(8,128)} %bitcast.23, ...), custom_call_target="tpu_custom_call" | custom-call | tf_op jit(solution)/shard_map/moe_bwd/pallas_call | solution.py:485
  121.8 3.1 %write_out.1 = (bf16[256,1024]{1,0:T(8,128)(2,1)}, f32[8,256]{1,0:T(8,128)}, f32[1024,512]{1,0:T(8,128)}, f32[1024,512]{1,0:T(8,128)}, f32[512,1024]{1,0:T(8,128)}) custom-call(bf16[256,1024]{1,0:T(8,128)(2,1)S(1)} %get-tuple-element.15.refs_0_, f32[8,256]{1,0:T(8,128)S(1)} %get-tuple-element.16.refs_1_, f32[1024,512]{1,0:T(8,128)S(1)} %get-tuple-element.17.refs_2_, ...), custom_call_target="tpu_custom_call" | custom-call | tf_op jit(solution)/shard_map/write_out/pallas_call | solution.py:534

commit v8 on v7

--- a/solution.py
+++ b/solution.py
@@ -27,7 +27,6 @@
 RELAY = {15: (11,)}
 TAIL_RELAY = (13, 10, 8, 14), (15, 12)
 
-PIECE = 512 * 1024
 LINES = (2, 0, -1, 1)
 PART = {2: 0, 1: 1, -1: 2, 0: 3}
 
@@ -52,7 +51,7 @@
            gx_ref, gg_ref, gwg_ref, gwu_ref, gwd_ref,
            tokens, stab, tabs, mids, mslots, rbuf, ret, relay, part, hop_in, fin, wgu, wd, xb, hgb, hub,
            tok_sem, tab_sem, meta_sem, ret_sem, relay_sem, hop_sem, fin_sem,
-           ag_send, pair_send, tab_send, meta_send, ret_send, relay_send, part_send, load_sem, w_sem, round_sem):
+           ag_send, pair_send, tab_send, meta_send, ret_send, relay_send, part_send, load_sem, w_sem, round_sem, gates, counts, in_sem):
     me = lax.axis_index("ep")
     core = me % CORES
     mx = (me // CORES) % side
@@ -93,19 +92,21 @@
     barrier = pltpu.get_barrier_semaphore()
     tell(barrier)
 
+    own_copies = [
+        pltpu.make_async_copy(gy_ref, tokens.at[me], in_sem.at[0]),
+        pltpu.make_async_copy(ids_ref, mids.at[my_b], in_sem.at[1]),
+        pltpu.make_async_copy(slots_ref, mslots.at[my_b], in_sem.at[2]),
+        pltpu.make_async_copy(gates_ref, gates, in_sem.at[3]),
+        pltpu.make_async_copy(pc_ref, counts, in_sem.at[4]),
+    ]
+    for c in own_copies:
+        c.start()
     wcopies = [
         pltpu.make_async_copy(wd_ref, wd, w_sem.at[0]),
         pltpu.make_async_copy(wg_ref, wgu.at[:, pl.ds(0, ffn)], w_sem.at[1]),
         pltpu.make_async_copy(wu_ref, wgu.at[:, pl.ds(ffn, ffn)], w_sem.at[2]),
     ]
     for c in wcopies:
-        c.start()
-    own_copies = [
-        pltpu.make_async_copy(gy_ref, tokens.at[me], tok_sem.at[me, 0]),
-        pltpu.make_async_copy(ids_ref, mids.at[my_b], meta_sem.at[my_b, 0]),
-        pltpu.make_async_copy(slots_ref, mslots.at[my_b], meta_sem.at[my_b, 1]),
-    ]
-    for c in own_copies:
         c.start()
 
     def offset(k, axis):
@@ -124,18 +125,63 @@
             pltpu.make_async_copy(hu_ref.at[rows], hub.at[slot], load_sem.at[2, slot]),
         ]
 
+    pl.semaphore_wait(barrier, len(peers))
+    own_copies[0].wait()
+
+    sends, pairs = [], []
+
+    def block(src, h):
+        return tokens.at[src, pl.ds(h * half, half)]
+
+    def forward_msg(n, i, j, h, a, b):
+        src = plane(i, j)
+        return remote(block(src, h), block(src, h), ag_send.at[n], tok_sem.at[src, h], plane(a, b))
+
+    def forward(*what):
+        what = (len(sends), *what)
+        sends.append(what)
+        forward_msg(*what).start()
+
+    def pair_msg(n, i, j):
+        src = plane(i, j)
+        return remote(tokens.at[src], tokens.at[src], pair_send.at[n], tok_sem.at[src, 0], partner)
+
+    def to_partner(i, j):
+        what = (len(pairs), i, j)
+        pairs.append(what)
+        pair_msg(*what).start()
+
+    def arrived(src, h):
+        landed(block(src, h), tok_sem.at[src, h])
+
+    to_partner(0, 0)
+
+    def tab_msg(i):
+        to = (me + 1 + i) % n_dev
+        return remote(stab.at[to], tabs.at[me], tab_send.at[i], tab_sem.at[me], to)
+
+    def tab_start(i, carry):
+        tab_msg(i).start()
+        return carry
+
+    for n in range(2):
+        for a, b, h in ((1, 0, n), (-1, 0, 1 - n), (0, 1, n), (0, -1, 1 - n)):
+            forward(0, 0, h, a, b)
+
+    tell(round_sem.at[0])
     for c in loads(0):
         c.start()
 
-    ids = ids_ref[...]
-    slots = slots_ref[...]
-    gates = gates_ref[...]
+    for c in own_copies[1:]:
+        c.wait()
+    ids = mids[my_b]
+    slots = mslots[my_b]
 
     def table(e, carry):
         hit = ids == e
         slot = jnp.max(jnp.where(hit, slots, -1), axis=0, keepdims=True)
-        slot = jnp.where(slot < pc_ref[0, e], slot, -1)
-        gate = jnp.sum(jnp.where(hit, gates, 0.0), axis=0, keepdims=True)
+        slot = jnp.where(slot < counts[0, e], slot, -1)
+        gate = jnp.sum(jnp.where(hit, gates[...], 0.0), axis=0, keepdims=True)
         stab[e] = jnp.concatenate([slot.astype(F32), gate], axis=0)
         return carry
 
@@ -143,51 +189,10 @@
     gwg_ref[...] = jnp.zeros_like(gwg_ref)
     gwu_ref[...] = jnp.zeros_like(gwu_ref)
     gwd_ref[...] = jnp.zeros_like(gwd_ref)
-    pl.semaphore_wait(barrier, len(peers))
-    own_copies[0].wait()
-
-    sends, pairs = [], []
-
-    def block(src, h):
-        return tokens.at[src, pl.ds(h * half, half)]
-
-    def forward_msg(n, i, j, h, a, b):
-        src = plane(i, j)
-        return remote(block(src, h), block(src, h), ag_send.at[n], tok_sem.at[src, h], plane(a, b))
-
-    def forward(*what):
-        what = (len(sends), *what)
-        sends.append(what)
-        forward_msg(*what).start()
-
-    def pair_msg(n, i, j):
-        src = plane(i, j)
-        return remote(tokens.at[src], tokens.at[src], pair_send.at[n], tok_sem.at[src, 0], partner)
-
-    def to_partner(i, j):
-        what = (len(pairs), i, j)
-        pairs.append(what)
-        pair_msg(*what).start()
-
-    def arrived(src, h):
-        landed(block(src, h), tok_sem.at[src, h])
-
-    to_partner(0, 0)
-
-    def tab_msg(i):
-        to = (me + 1 + i) % n_dev
-        return remote(stab.at[to], tabs.at[me], tab_send.at[i], tab_sem.at[me], to)
-
-    def tab_start(i, carry):
-        tab_msg(i).start()
-        return carry
-
-    for n in range(2):
-        for a, b, h in ((1, 0, n), (-1, 0, 1 - n), (0, 1, n), (0, -1, 1 - n)):
-            forward(0, 0, h, a, b)
 
     for n in range(side - 1):
-        tell(round_sem.at[n])
+        if n:
+            tell(round_sem.at[n])
         pl.semaphore_wait(round_sem.at[n], len(peers))
     lax.fori_loop(0, n_dev - 1, tab_start, 0)
     tab_copy = pltpu.make_async_copy(stab.at[me], tabs.at[me], tab_sem.at[me])
@@ -195,8 +200,8 @@
     def meta_msgs():
         out = []
         for n, j in enumerate((1, -1, 2)):
-            out.append(remote(ids_ref, mids.at[my_b], meta_send.at[n, 0], meta_sem.at[my_b, 0], plane(0, j)))
-            out.append(remote(slots_ref, mslots.at[my_b], meta_send.at[n, 1], meta_sem.at[my_b, 1], plane(0, j)))
+            out.append(remote(mids.at[my_b], mids.at[my_b], meta_send.at[n, 0], meta_sem.at[my_b, 0], plane(0, j)))
+            out.append(remote(mslots.at[my_b], mslots.at[my_b], meta_send.at[n, 1], meta_sem.at[my_b, 1], plane(0, j)))
         return out
 
     for c in meta_msgs():
@@ -362,8 +367,12 @@
     def add_rows(n, carry):
         j = lut(n, LINES)
         hb = wrap(my_b + j)
-        landed(mids.at[hb], meta_sem.at[hb, 0])
-        landed(mslots.at[hb], meta_sem.at[hb, 1])
+
+        @pl.when(j != 0)
+        def _():
+            landed(mids.at[hb], meta_sem.at[hb, 0])
+            landed(mslots.at[hb], meta_sem.at[hb, 1])
+
         h_ids = mids[hb]
         h_slots = mslots[hb]
         picks = []
@@ -449,13 +458,7 @@
 def write_out(*refs):
     n = len(refs) // 2
     sems = refs[-1]
-    copies = []
-    for i in range(n):
-        src, dst = refs[i], refs[n + i]
-        rows = src.shape[0]
-        step = max(8, min(rows, PIECE // (src.shape[1] * src.dtype.itemsize)))
-        for r in range(0, rows, step):
-            copies.append(pltpu.make_async_copy(src.at[pl.ds(r, step)], dst.at[pl.ds(r, step)], sems.at[len(copies)]))
+    copies = [pltpu.make_async_copy(refs[i], refs[n + i], sems.at[i]) for i in range(n)]
     for c in copies:
         c.start()
     for c in copies:
@@ -479,7 +482,6 @@
         n_chip = side * side
         top_k = topk_idx.shape[1]
         vmem = pl.BlockSpec(memory_space=pltpu.VMEM)
-        smem = pl.BlockSpec(memory_space=pltpu.SMEM)
         anym = pl.BlockSpec(memory_space=pl.ANY)
         dma = pltpu.SemaphoreType.DMA
         results = pl.pallas_call(
@@ -491,7 +493,7 @@
                 pltpu.VMEM((model_dim, ffn), F32),
                 pltpu.VMEM((ffn, model_dim), F32),
             ),
-            in_specs=[anym, vmem, vmem, vmem, smem] + [anym] * 7,
+            in_specs=[anym] * 12,
             out_specs=(vmem,) * 5,
             scratch_shapes=[
                 pltpu.VMEM((n_dev, tok_dev, model_dim), BF16),
@@ -527,6 +529,9 @@
                 dma((3, 2)),
                 dma((3,)),
                 pltpu.SemaphoreType.REGULAR((side - 1,)),
+                pltpu.VMEM((top_k, tok_dev), F32),
+                pltpu.SMEM(pair_counts.shape, jnp.int32),
+                dma((5,)),
             ],
             compiler_params=pltpu.CompilerParams(collective_id=0, has_side_effects=True, vmem_limit_bytes=58720256),
             name="moe_bwd",
@@ -536,7 +541,7 @@
             out_shape=tuple(jax.ShapeDtypeStruct(r.shape, r.dtype) for r in results),
             in_specs=[anym] * len(results),
             out_specs=(anym,) * len(results),
-            scratch_shapes=[dma((32,))],
+            scratch_shapes=[dma((len(results),))],
             compiler_params=pltpu.CompilerParams(vmem_limit_bytes=1048576),
             name="write_out",
         )(*results)

time: 125 us -> 124 us (level)
  no operation moved by 1% of the time
where the time goes in v8:
time: 124 us
  Pallas kernels  123 us (99%)
    pallas_call x1, Pallas kernels, local_step(): pl.pallas_call(functools.partial(kernel, n_dev, side), out_shape=(pltpu.V...  120 us
    pallas_call x1, Pallas kernels, local_step(): pl.pallas_call(write_out, out_shape=tuple((jax.ShapeDtypeStruct(r.shape,...  2.92 us

profile of v8, /device:TPU:97, one launch (start us, length us, event | category | flops | bytes accessed | tf_op | source)
XLA Modules:
  0.0 123.8 jit_solution(6561511433721599587)
XLA Ops:
  0.6 120.3 %moe_bwd.1 = (bf16[256,1024]{1,0:T(8,128)(2,1)S(1)}, f32[8,256]{1,0:T(8,128)S(1)}, f32[1024,512]{1,0:T(8,128)S(1)}, f32[1024,512]{1,0:T(8,128)S(1)}, f32[512,1024]{1,0:T(8,128)S(1)}) custom-call(bf16[256,1024]{1,0:T(8,128)(2,1)} %gy_ref.1, s32[8,256]{1,0:T(8,128)} %bitcast.21, s32[8,256]{1,0:T(8,128)} %bitcast.22, f32[8,256]{1,0:T(8,128)} %bitcast.23, ...), custom_call_target="tpu_custom_call" | custom-call | tf_op jit(solution)/shard_map/moe_bwd/pallas_call | solution.py:487
  120.9 2.9 %write_out.1 = (bf16[256,1024]{1,0:T(8,128)(2,1)}, f32[8,256]{1,0:T(8,128)}, f32[1024,512]{1,0:T(8,128)}, f32[1024,512]{1,0:T(8,128)}, f32[512,1024]{1,0:T(8,128)}) custom-call(bf16[256,1024]{1,0:T(8,128)(2,1)S(1)} %get-tuple-element.15.refs_0_, f32[8,256]{1,0:T(8,128)S(1)} %get-tuple-element.16.refs_1_, f32[1024,512]{1,0:T(8,128)S(1)} %get-tuple-element.17.refs_2_, ...), custom_call_target="tpu_custom_call" | custom-call | tf_op jit(solution)/shard_map/write_out/pallas_call | solution.py:539

commit v9 on v8

--- a/solution.py
+++ b/solution.py
@@ -12,22 +12,24 @@
 CORES = 2
 BF16, F32 = jnp.bfloat16, jnp.float32
 
-ORDER = ((-1, 0), (0, 1), (0, -1), (0, 0), (-1, 1), (1, 0), (1, -1), (1, 1), (0, 2), (-1, -1), (2, 0), (2, 1), (2, -1), (2, 2), (1, 2), (-1, 2))
+ORDER = ((0, 0), (-1, 0), (0, 1), (1, 0), (0, -1), (1, -1), (-1, 1), (1, 1), (0, 2), (2, 0), (-1, 2), (2, -1), (2, 1), (-1, -1), (2, 2), (1, 2))
 EVENTS = {
-    0: ((-1, 0), (0, -1), (1, 0), (0, 1)),
-    2: ((2, 0), (-1, 1)),
-    4: ((0, 2), (1, -1), (-1, -1)),
-    5: ((1, 1),),
+    0: ((-1, 0), (0, 1), (1, 0)),
+    1: ((0, -1),),
+    2: ((1, -1), (-1, -1), (2, 0)),
+    4: ((1, 1), (-1, 1)),
     6: ((2, -1),),
-    9: ((2, 1),),
+    7: ((0, 2),),
+    8: ((2, 1),),
+    9: ((-1, 2),),
     10: ((1, 2),),
-    12: ((2, 2), (-1, 2)),
+    13: ((2, 2),),
 }
 FLIP = 1
-RELAY = {15: (11,)}
-TAIL_RELAY = (13, 10, 8, 14), (15, 12)
-
-LINES = (2, 0, -1, 1)
+RELAY = {14: (9,), 15: (11, 10)}
+TAIL_RELAY = (14, 8), (12, 15)
+
+LINES = (-1, 2, 1, 0)
 PART = {2: 0, 1: 1, -1: 2, 0: 3}
 
 NN = (((1,), (0,)), ((), ()))
@@ -274,15 +276,15 @@
         c.wait()
 
     def chunk(k, carry):
+        @pl.when(k > 0)
+        def _():
+            send_chunk(k - 1)
+
         for at, evs in EVENTS.items():
             @pl.when(k == at)
             def _(evs=evs):
                 for i, j in evs:
                     event(i, j)
-
-        @pl.when(k > 0)
-        def _():
-            send_chunk(k - 1)
 
         for at, steps in RELAY.items():
             @pl.when(k == at)
@@ -378,21 +380,23 @@
         picks = []
         for sa in range(side):
             for ce in range(CORES):
-                slot = (hb * side + sa) * CORES + ce
-                landed(ret.at[slot], ret_sem.at[slot])
                 x = (1 - turn) * sa + turn * my_b
                 y = (1 - turn) * my_b + turn * sa
                 row = jnp.max(jnp.where(h_ids == (y * side + x) * CORES + ce, h_slots, -1), axis=0, keepdims=True)
                 picks.append((row == slot_iota).astype(F32).astype(BF16))
         pick = jnp.concatenate(picks, axis=0)
-        rows = ret[pl.ds(hb * side * CORES, side * CORES)].reshape(side * CORES * cap, model_dim)
-        part[lut(n, [PART[v] for v in LINES])] = dot(pick, rows, TN)
-
-        @pl.when(n == 1)
+
+        @pl.when(n == 2)
         def _():
             for c in hop_msgs():
                 c.start()
 
+        for sa in range(side):
+            for ce in range(CORES):
+                slot = (hb * side + sa) * CORES + ce
+                landed(ret.at[slot], ret_sem.at[slot])
+        rows = ret[pl.ds(hb * side * CORES, side * CORES)].reshape(side * CORES * cap, model_dim)
+        part[lut(n, [PART[v] for v in LINES])] = dot(pick, rows, TN)
         return carry
 
     def hop_msgs():
@@ -411,11 +415,11 @@
     fins = fin_msgs()
     lax.fori_loop(0, len(LINES), add_rows, 0)
     fins[2].start()
+    fins[1].start()
     for what in sends:
         forward_msg(*what).wait_send()
     for what in pairs:
         pair_msg(*what).wait_send()
-    fins[1].start()
     landed(hop_in.at[0], hop_sem.at[0])
     part[1, pl.ds(0, half)] += hop_in[0]
     landed(hop_in.at[1], hop_sem.at[1])

time: 124 us -> 130 us (1.048)
  Pallas kernels: 123 us -> 129 us
    pallas_call x1, Pallas kernels: 120 us -> 126 us  [local_step(): pl.pallas_call(functools.partial(kernel, n_dev, side), out_shape=(pltpu.V...]
where the time goes in v9:
time: 130 us; the launch traced here: 129 us
  Pallas kernels  129 us (99%)
    pallas_call x1, Pallas kernels, local_step(): pl.pallas_call(functools.partial(kernel, n_dev, side), out_shape=(pltpu.V...  126 us
    pallas_call x1, Pallas kernels, local_step(): pl.pallas_call(write_out, out_shape=tuple((jax.ShapeDtypeStruct(r.shape,...  2.92 us

profile of v9, /device:TPU:97, one launch (start us, length us, event | category | flops | bytes accessed | tf_op | source)
XLA Modules:
  0.0 129.5 jit_solution(4399350236669292164)
XLA Ops:
  0.6 125.9 %moe_bwd.1 = (bf16[256,1024]{1,0:T(8,128)(2,1)S(1)}, f32[8,256]{1,0:T(8,128)S(1)}, f32[1024,512]{1,0:T(8,128)S(1)}, f32[1024,512]{1,0:T(8,128)S(1)}, f32[512,1024]{1,0:T(8,128)S(1)}) custom-call(bf16[256,1024]{1,0:T(8,128)(2,1)} %gy_ref.1, s32[8,256]{1,0:T(8,128)} %bitcast.21, s32[8,256]{1,0:T(8,128)} %bitcast.22, f32[8,256]{1,0:T(8,128)} %bitcast.23, ...), custom_call_target="tpu_custom_call" | custom-call | tf_op jit(solution)/shard_map/moe_bwd/pallas_call | solution.py:491
  126.6 2.9 %write_out.1 = (bf16[256,1024]{1,0:T(8,128)(2,1)}, f32[8,256]{1,0:T(8,128)}, f32[1024,512]{1,0:T(8,128)}, f32[1024,512]{1,0:T(8,128)}, f32[512,1024]{1,0:T(8,128)}) custom-call(bf16[256,1024]{1,0:T(8,128)(2,1)S(1)} %get-tuple-element.15.refs_0_, f32[8,256]{1,0:T(8,128)S(1)} %get-tuple-element.16.refs_1_, f32[1024,512]{1,0:T(8,128)S(1)} %get-tuple-element.17.refs_2_, ...), custom_call_target="tpu_custom_call" | custom-call | tf_op jit(solution)/shard_map/write_out/pallas_call | solution.py:543

commit v10 on v8

--- a/solution.py
+++ b/solution.py
@@ -274,15 +274,15 @@
         c.wait()
 
     def chunk(k, carry):
+        @pl.when(k > 0)
+        def _():
+            send_chunk(k - 1)
+
         for at, evs in EVENTS.items():
             @pl.when(k == at)
             def _(evs=evs):
                 for i, j in evs:
                     event(i, j)
-
-        @pl.when(k > 0)
-        def _():
-            send_chunk(k - 1)
 
         for at, steps in RELAY.items():
             @pl.when(k == at)

time: 124 us -> 123 us (level)
  no operation moved by 1% of the time
where the time goes in v10:
time: 123 us
  Pallas kernels  122 us (99%)
    pallas_call x1, Pallas kernels, local_step(): pl.pallas_call(functools.partial(kernel, n_dev, side), out_shape=(pltpu.V...  119 us
    pallas_call x1, Pallas kernels, local_step(): pl.pallas_call(write_out, out_shape=tuple((jax.ShapeDtypeStruct(r.shape,...  2.92 us

profile of v10, /device:TPU:97, one launch (start us, length us, event | category | flops | bytes accessed | tf_op | source)
XLA Modules:
  0.0 122.6 jit_solution(16231589205614666962)
XLA Ops:
  0.6 119.1 %moe_bwd.1 = (bf16[256,1024]{1,0:T(8,128)(2,1)S(1)}, f32[8,256]{1,0:T(8,128)S(1)}, f32[1024,512]{1,0:T(8,128)S(1)}, f32[1024,512]{1,0:T(8,128)S(1)}, f32[512,1024]{1,0:T(8,128)S(1)}) custom-call(bf16[256,1024]{1,0:T(8,128)(2,1)} %gy_ref.1, s32[8,256]{1,0:T(8,128)} %bitcast.21, s32[8,256]{1,0:T(8,128)} %bitcast.22, f32[8,256]{1,0:T(8,128)} %bitcast.23, ...), custom_call_target="tpu_custom_call" | custom-call | tf_op jit(solution)/shard_map/moe_bwd/pallas_call | solution.py:487
  119.7 2.9 %write_out.1 = (bf16[256,1024]{1,0:T(8,128)(2,1)}, f32[8,256]{1,0:T(8,128)}, f32[1024,512]{1,0:T(8,128)}, f32[1024,512]{1,0:T(8,128)}, f32[512,1024]{1,0:T(8,128)}) custom-call(bf16[256,1024]{1,0:T(8,128)(2,1)S(1)} %get-tuple-element.15.refs_0_, f32[8,256]{1,0:T(8,128)S(1)} %get-tuple-element.16.refs_1_, f32[1024,512]{1,0:T(8,128)S(1)} %get-tuple-element.17.refs_2_, ...), custom_call_target="tpu_custom_call" | custom-call | tf_op jit(solution)/shard_map/write_out/pallas_call | solution.py:539

commit v11 on v10

--- a/solution.py
+++ b/solution.py
@@ -24,8 +24,8 @@
     12: ((2, 2), (-1, 2)),
 }
 FLIP = 1
-RELAY = {15: (11,)}
-TAIL_RELAY = (13, 10, 8, 14), (15, 12)
+RELAY = {}
+TAIL_RELAY = (11, 13, 10, 8, 14), (15, 12)
 
 LINES = (2, 0, -1, 1)
 PART = {2: 0, 1: 1, -1: 2, 0: 3}
@@ -378,21 +378,23 @@
         picks = []
         for sa in range(side):
             for ce in range(CORES):
-                slot = (hb * side + sa) * CORES + ce
-                landed(ret.at[slot], ret_sem.at[slot])
                 x = (1 - turn) * sa + turn * my_b
                 y = (1 - turn) * my_b + turn * sa
                 row = jnp.max(jnp.where(h_ids == (y * side + x) * CORES + ce, h_slots, -1), axis=0, keepdims=True)
                 picks.append((row == slot_iota).astype(F32).astype(BF16))
         pick = jnp.concatenate(picks, axis=0)
-        rows = ret[pl.ds(hb * side * CORES, side * CORES)].reshape(side * CORES * cap, model_dim)
-        part[lut(n, [PART[v] for v in LINES])] = dot(pick, rows, TN)
 
         @pl.when(n == 1)
         def _():
             for c in hop_msgs():
                 c.start()
 
+        for sa in range(side):
+            for ce in range(CORES):
+                slot = (hb * side + sa) * CORES + ce
+                landed(ret.at[slot], ret_sem.at[slot])
+        rows = ret[pl.ds(hb * side * CORES, side * CORES)].reshape(side * CORES * cap, model_dim)
+        part[lut(n, [PART[v] for v in LINES])] = dot(pick, rows, TN)
         return carry
 
     def hop_msgs():

time: 123 us -> 124 us (level)
  no operation moved by 1% of the time
where the time goes in v11:
time: 124 us; the launch traced here: 123 us
  Pallas kernels  123 us (99%)
    pallas_call x1, Pallas kernels, local_step(): pl.pallas_call(functools.partial(kernel, n_dev, side), out_shape=(pltpu.V...  120 us
    pallas_call x1, Pallas kernels, local_step(): pl.pallas_call(write_out, out_shape=tuple((jax.ShapeDtypeStruct(r.shape,...  2.92 us

profile of v11, /device:TPU:97, one launch (start us, length us, event | category | flops | bytes accessed | tf_op | source)
XLA Modules:
  0.0 123.2 jit_solution(10295458514724776827)
XLA Ops:
  0.6 119.6 %moe_bwd.1 = (bf16[256,1024]{1,0:T(8,128)(2,1)S(1)}, f32[8,256]{1,0:T(8,128)S(1)}, f32[1024,512]{1,0:T(8,128)S(1)}, f32[1024,512]{1,0:T(8,128)S(1)}, f32[512,1024]{1,0:T(8,128)S(1)}) custom-call(bf16[256,1024]{1,0:T(8,128)(2,1)} %gy_ref.1, s32[8,256]{1,0:T(8,128)} %bitcast.21, s32[8,256]{1,0:T(8,128)} %bitcast.22, f32[8,256]{1,0:T(8,128)} %bitcast.23, ...), custom_call_target="tpu_custom_call" | custom-call | tf_op jit(solution)/shard_map/moe_bwd/pallas_call | solution.py:489
  120.2 2.9 %write_out.1 = (bf16[256,1024]{1,0:T(8,128)(2,1)}, f32[8,256]{1,0:T(8,128)}, f32[1024,512]{1,0:T(8,128)}, f32[1024,512]{1,0:T(8,128)}, f32[512,1024]{1,0:T(8,128)}) custom-call(bf16[256,1024]{1,0:T(8,128)(2,1)S(1)} %get-tuple-element.15.refs_0_, f32[8,256]{1,0:T(8,128)S(1)} %get-tuple-element.16.refs_1_, f32[1024,512]{1,0:T(8,128)S(1)} %get-tuple-element.17.refs_2_, ...), custom_call_target="tpu_custom_call" | custom-call | tf_op jit(solution)/shard_map/write_out/pallas_call | solution.py:541

commit v12 on v9

--- a/solution.py
+++ b/solution.py
@@ -12,24 +12,23 @@
 CORES = 2
 BF16, F32 = jnp.bfloat16, jnp.float32
 
-ORDER = ((0, 0), (-1, 0), (0, 1), (1, 0), (0, -1), (1, -1), (-1, 1), (1, 1), (0, 2), (2, 0), (-1, 2), (2, -1), (2, 1), (-1, -1), (2, 2), (1, 2))
+ORDER = ((1, 0), (0, 0), (-1, 0), (1, 1), (0, 2), (0, -1), (2, 0), (0, 1), (-1, -1), (1, -1), (-1, 1), (2, 1), (2, -1), (2, 2), (1, 2), (-1, 2))
 EVENTS = {
-    0: ((-1, 0), (0, 1), (1, 0)),
-    1: ((0, -1),),
-    2: ((1, -1), (-1, -1), (2, 0)),
-    4: ((1, 1), (-1, 1)),
-    6: ((2, -1),),
-    7: ((0, 2),),
-    8: ((2, 1),),
-    9: ((-1, 2),),
-    10: ((1, 2),),
+    0: ((1, 0), (-1, 0), (0, 1), (0, -1)),
+    1: ((1, -1), (1, 1)),
+    2: ((2, 0),),
+    4: ((0, 2), (-1, -1)),
+    6: ((-1, 1), (2, 1)),
+    7: ((1, 2),),
+    9: ((2, -1),),
+    11: ((-1, 2),),
     13: ((2, 2),),
 }
 FLIP = 1
-RELAY = {14: (9,), 15: (11, 10)}
-TAIL_RELAY = (14, 8), (12, 15)
-
-LINES = (-1, 2, 1, 0)
+RELAY = {10: (4,), 13: (6,), 15: (11,)}
+TAIL_RELAY = (13, 14), (15, 12)
+
+LINES = (0, 2, 1, -1)
 PART = {2: 0, 1: 1, -1: 2, 0: 3}
 
 NN = (((1,), (0,)), ((), ()))
@@ -414,12 +413,12 @@
 
     fins = fin_msgs()
     lax.fori_loop(0, len(LINES), add_rows, 0)
-    fins[2].start()
     fins[1].start()
     for what in sends:
         forward_msg(*what).wait_send()
     for what in pairs:
         pair_msg(*what).wait_send()
+    fins[2].start()
     landed(hop_in.at[0], hop_sem.at[0])
     part[1, pl.ds(0, half)] += hop_in[0]
     landed(hop_in.at[1], hop_sem.at[1])

time: 130 us -> 125 us (0.962)
  Pallas kernels: 129 us -> 124 us
    pallas_call x1, Pallas kernels: 126 us -> 121 us  [local_step(): pl.pallas_call(functools.partial(kernel, n_dev, side), out_shape=(pltpu.V...]
where the time goes in v12:
time: 125 us
  Pallas kernels  124 us (99%)
    pallas_call x1, Pallas kernels, local_step(): pl.pallas_call(functools.partial(kernel, n_dev, side), out_shape=(pltpu.V...  121 us
    pallas_call x1, Pallas kernels, local_step(): pl.pallas_call(write_out, out_shape=tuple((jax.ShapeDtypeStruct(r.shape,...  2.92 us

profile of v12, /device:TPU:97, one launch (start us, length us, event | category | flops | bytes accessed | tf_op | source)
XLA Modules:
  0.0 124.9 jit_solution(1894270377363846438)
XLA Ops:
  0.6 121.4 %moe_bwd.1 = (bf16[256,1024]{1,0:T(8,128)(2,1)S(1)}, f32[8,256]{1,0:T(8,128)S(1)}, f32[1024,512]{1,0:T(8,128)S(1)}, f32[1024,512]{1,0:T(8,128)S(1)}, f32[512,1024]{1,0:T(8,128)S(1)}) custom-call(bf16[256,1024]{1,0:T(8,128)(2,1)} %gy_ref.1, s32[8,256]{1,0:T(8,128)} %bitcast.21, s32[8,256]{1,0:T(8,128)} %bitcast.22, f32[8,256]{1,0:T(8,128)} %bitcast.23, ...), custom_call_target="tpu_custom_call" | custom-call | tf_op jit(solution)/shard_map/moe_bwd/pallas_call | solution.py:490
  122.0 2.9 %write_out.1 = (bf16[256,1024]{1,0:T(8,128)(2,1)}, f32[8,256]{1,0:T(8,128)}, f32[1024,512]{1,0:T(8,128)}, f32[1024,512]{1,0:T(8,128)}, f32[512,1024]{1,0:T(8,128)}) custom-call(bf16[256,1024]{1,0:T(8,128)(2,1)S(1)} %get-tuple-element.15.refs_0_, f32[8,256]{1,0:T(8,128)S(1)} %get-tuple-element.16.refs_1_, f32[1024,512]{1,0:T(8,128)S(1)} %get-tuple-element.17.refs_2_, ...), custom_call_target="tpu_custom_call" | custom-call | tf_op jit(solution)/shard_map/write_out/pallas_call | solution.py:542

commit v13 on v10

--- a/solution.py
+++ b/solution.py
@@ -12,7 +12,7 @@
 CORES = 2
 BF16, F32 = jnp.bfloat16, jnp.float32
 
-ORDER = ((-1, 0), (0, 1), (0, -1), (0, 0), (-1, 1), (1, 0), (1, -1), (1, 1), (0, 2), (-1, -1), (2, 0), (2, 1), (2, -1), (2, 2), (1, 2), (-1, 2))
+ORDER = ((0, -1), (1, 0), (-1, 0), (0, 0), (1, -1), (0, 1), (-1, 1), (1, 1), (2, 0), (-1, -1), (0, 2), (1, 2), (-1, 2), (2, 2), (2, 1), (2, -1))
 EVENTS = {
     0: ((-1, 0), (0, -1), (1, 0), (0, 1)),
     2: ((2, 0), (-1, 1)),
@@ -23,7 +23,7 @@
     10: ((1, 2),),
     12: ((2, 2), (-1, 2)),
 }
-FLIP = 1
+FLIP = 0
 RELAY = {15: (11,)}
 TAIL_RELAY = (13, 10, 8, 14), (15, 12)
 

time: 123 us -> 124 us (level)
  no operation moved by 1% of the time
where the time goes in v13:
time: 124 us; the launch traced here: 123 us
  Pallas kernels  123 us (99%)
    pallas_call x1, Pallas kernels, local_step(): pl.pallas_call(functools.partial(kernel, n_dev, side), out_shape=(pltpu.V...  120 us
    pallas_call x1, Pallas kernels, local_step(): pl.pallas_call(write_out, out_shape=tuple((jax.ShapeDtypeStruct(r.shape,...  2.92 us

profile of v13, /device:TPU:97, one launch (start us, length us, event | category | flops | bytes accessed | tf_op | source)
XLA Modules:
  0.0 123.4 jit_solution(8064018092509870508)
XLA Ops:
  0.6 119.8 %moe_bwd.1 = (bf16[256,1024]{1,0:T(8,128)(2,1)S(1)}, f32[8,256]{1,0:T(8,128)S(1)}, f32[1024,512]{1,0:T(8,128)S(1)}, f32[1024,512]{1,0:T(8,128)S(1)}, f32[512,1024]{1,0:T(8,128)S(1)}) custom-call(bf16[256,1024]{1,0:T(8,128)(2,1)} %gy_ref.1, s32[8,256]{1,0:T(8,128)} %bitcast.21, s32[8,256]{1,0:T(8,128)} %bitcast.22, f32[8,256]{1,0:T(8,128)} %bitcast.23, ...), custom_call_target="tpu_custom_call" | custom-call | tf_op jit(solution)/shard_map/moe_bwd/pallas_call | solution.py:487
  120.5 2.9 %write_out.1 = (bf16[256,1024]{1,0:T(8,128)(2,1)}, f32[8,256]{1,0:T(8,128)}, f32[1024,512]{1,0:T(8,128)}, f32[1024,512]{1,0:T(8,128)}, f32[512,1024]{1,0:T(8,128)}) custom-call(bf16[256,1024]{1,0:T(8,128)(2,1)S(1)} %get-tuple-element.15.refs_0_, f32[8,256]{1,0:T(8,128)S(1)} %get-tuple-element.16.refs_1_, f32[1024,512]{1,0:T(8,128)S(1)} %get-tuple-element.17.refs_2_, ...), custom_call_target="tpu_custom_call" | custom-call | tf_op jit(solution)/shard_map/write_out/pallas_call | solution.py:539

commit v14 on v10

--- a/solution.py
+++ b/solution.py
@@ -24,8 +24,8 @@
     12: ((2, 2), (-1, 2)),
 }
 FLIP = 1
-RELAY = {15: (11,)}
-TAIL_RELAY = (13, 10, 8, 14), (15, 12)
+RELAY = {14: (8, 10), 15: (11,)}
+TAIL_RELAY = (13, 14), (15, 12)
 
 LINES = (2, 0, -1, 1)
 PART = {2: 0, 1: 1, -1: 2, 0: 3}

time: 123 us -> 128 us (1.041); the launches traced: 123 us -> 126 us
  Pallas kernels: 122 us -> 125 us
    pallas_call x1, Pallas kernels: 119 us -> 122 us  [local_step(): pl.pallas_call(functools.partial(kernel, n_dev, side), out_shape=(pltpu.V...]
where the time goes in v14:
time: 128 us; the launch traced here: 126 us
  Pallas kernels  125 us (98%)
    pallas_call x1, Pallas kernels, local_step(): pl.pallas_call(functools.partial(kernel, n_dev, side), out_shape=(pltpu.V...  122 us
    pallas_call x1, Pallas kernels, local_step(): pl.pallas_call(write_out, out_shape=tuple((jax.ShapeDtypeStruct(r.shape,...  2.92 us

profile of v14, /device:TPU:97, one launch (start us, length us, event | category | flops | bytes accessed | tf_op | source)
XLA Modules:
  0.0 126.0 jit_solution(17348729475067603030)
XLA Ops:
  0.6 122.4 %moe_bwd.1 = (bf16[256,1024]{1,0:T(8,128)(2,1)S(1)}, f32[8,256]{1,0:T(8,128)S(1)}, f32[1024,512]{1,0:T(8,128)S(1)}, f32[1024,512]{1,0:T(8,128)S(1)}, f32[512,1024]{1,0:T(8,128)S(1)}) custom-call(bf16[256,1024]{1,0:T(8,128)(2,1)} %gy_ref.1, s32[8,256]{1,0:T(8,128)} %bitcast.21, s32[8,256]{1,0:T(8,128)} %bitcast.22, f32[8,256]{1,0:T(8,128)} %bitcast.23, ...), custom_call_target="tpu_custom_call" | custom-call | tf_op jit(solution)/shard_map/moe_bwd/pallas_call | solution.py:487
  123.1 2.9 %write_out.1 = (bf16[256,1024]{1,0:T(8,128)(2,1)}, f32[8,256]{1,0:T(8,128)}, f32[1024,512]{1,0:T(8,128)}, f32[1024,512]{1,0:T(8,128)}, f32[512,1024]{1,0:T(8,128)}) custom-call(bf16[256,1024]{1,0:T(8,128)(2,1)S(1)} %get-tuple-element.15.refs_0_, f32[8,256]{1,0:T(8,128)S(1)} %get-tuple-element.16.refs_1_, f32[1024,512]{1,0:T(8,128)S(1)} %get-tuple-element.17.refs_2_, ...), custom_call_target="tpu_custom_call" | custom-call | tf_op jit(solution)/shard_map/write_out/pallas_call | solution.py:539

commit v15 on v14

--- a/solution.py
+++ b/solution.py
@@ -24,8 +24,8 @@
     12: ((2, 2), (-1, 2)),
 }
 FLIP = 1
-RELAY = {14: (8, 10), 15: (11,)}
-TAIL_RELAY = (13, 14), (15, 12)
+RELAY = {}
+TAIL_RELAY = (11, 13, 10, 8, 14), (15, 12)
 
 LINES = (2, 0, -1, 1)
 PART = {2: 0, 1: 1, -1: 2, 0: 3}

time: 128 us -> 124 us (0.969)
  Pallas kernels: 125 us -> 122 us
    pallas_call x1, Pallas kernels: 122 us -> 119 us  [local_step(): pl.pallas_call(functools.partial(kernel, n_dev, side), out_shape=(pltpu.V...]
where the time goes in v15:
time: 124 us; the launch traced here: 122 us
  Pallas kernels  122 us (98%)
    pallas_call x1, Pallas kernels, local_step(): pl.pallas_call(functools.partial(kernel, n_dev, side), out_shape=(pltpu.V...  119 us
    pallas_call x1, Pallas kernels, local_step(): pl.pallas_call(write_out, out_shape=tuple((jax.ShapeDtypeStruct(r.shape,...  2.92 us

profile of v15, /device:TPU:97, one launch (start us, length us, event | category | flops | bytes accessed | tf_op | source)
XLA Modules:
  0.0 122.4 jit_solution(2030279406610417541)
XLA Ops:
  0.6 118.8 %moe_bwd.1 = (bf16[256,1024]{1,0:T(8,128)(2,1)S(1)}, f32[8,256]{1,0:T(8,128)S(1)}, f32[1024,512]{1,0:T(8,128)S(1)}, f32[1024,512]{1,0:T(8,128)S(1)}, f32[512,1024]{1,0:T(8,128)S(1)}) custom-call(bf16[256,1024]{1,0:T(8,128)(2,1)} %gy_ref.1, s32[8,256]{1,0:T(8,128)} %bitcast.21, s32[8,256]{1,0:T(8,128)} %bitcast.22, f32[8,256]{1,0:T(8,128)} %bitcast.23, ...), custom_call_target="tpu_custom_call" | custom-call | tf_op jit(solution)/shard_map/moe_bwd/pallas_call | solution.py:487
  119.4 2.9 %write_out.1 = (bf16[256,1024]{1,0:T(8,128)(2,1)}, f32[8,256]{1,0:T(8,128)}, f32[1024,512]{1,0:T(8,128)}, f32[1024,512]{1,0:T(8,128)}, f32[512,1024]{1,0:T(8,128)}) custom-call(bf16[256,1024]{1,0:T(8,128)(2,1)S(1)} %get-tuple-element.15.refs_0_, f32[8,256]{1,0:T(8,128)S(1)} %get-tuple-element.16.refs_1_, f32[1024,512]{1,0:T(8,128)S(1)} %get-tuple-element.17.refs_2_, ...), custom_call_target="tpu_custom_call" | custom-call | tf_op jit(solution)/shard_map/write_out/pallas_call | solution.py:539
